TPU v7x, 256 devices: a 8x8x2 block of a 8x8x16 slice. The times are simulated.
256 devices in a mesh: frag: 2 (over z), grid: 128 (over y, x, core).
Axes of the slice: x: 8, y: 8, z: 2, core: 2. Of those that a mesh axis runs over, the one named last changes fastest.
The devices are a block of a 8x8x16 slice.
Arguments:
- psi: float32 [131072, 640], P(('frag', 'grid')), parts along dimension 0
- order: int32 [10], P('frag'), parts along dimension 0, may hold values from 0 to 4, each once
Outputs:
- orthonormal: float32 [131072, 640], P(('frag', 'grid')), parts along dimension 0
There are 2 independent parts, one for each index of `frag`. A program takes and returns all parts, laid end to end along the dimension named above; each array names one. Nothing has to cross between parts.
All inputs are finite; a program needn't handle non-finite values.
Results may differ from a plain program's by a relative error of at most 0.00012.
Values sent between devices are 32-bit elements; how exact they have to be, the bound alone decides.
No kernel may reach another device: no remote copies, remote signals or barrier semaphores. Data moves between devices by JAX's collectives and lax.ppermute only.
A program may use at most 64 MiB of HBM per device.

v0:
```python
import jax
import jax.numpy as jnp
from jax import lax
from jax.sharding import PartitionSpec as P

BLOCK = 128
NBLK = 5


def contract(left, right):
    return lax.dot_general(
        left,
        right,
        (((0,), (0,)), ((), ())),
        precision=lax.Precision.HIGHEST,
        preferred_element_type=jnp.float32,
    )


def matmul(left, right):
    return jnp.dot(left, right, precision=lax.Precision.HIGHEST, preferred_element_type=jnp.float32)


def factor_inverse(gram, width):
    lower = jnp.linalg.cholesky(gram)
    return lax.linalg.triangular_solve(
        lower, jnp.eye(width, dtype=gram.dtype), left_side=True, lower=True
    )


def local(psi, order):
    scale = jnp.float32(1.0 / (psi.shape[0] * lax.axis_size("grid")))
    rows = psi.shape[0]
    reordered = jnp.take(psi.reshape(rows, NBLK, BLOCK), order, axis=1).reshape(rows, NBLK * BLOCK)
    whole = lax.psum(contract(reordered, reordered) * scale, "grid")
    inverse = factor_inverse(whole, NBLK * BLOCK)
    basis = matmul(reordered, inverse.T).reshape(rows, NBLK, BLOCK)
    result = jnp.zeros((rows, NBLK, BLOCK), psi.dtype).at[:, order, :].set(basis)
    return result.reshape(rows, NBLK * BLOCK)


def solution(mesh):
    in_specs = (P(("frag", "grid"), None), P("frag"))
    out_specs = P(("frag", "grid"), None)
    return jax.shard_map(local, mesh=mesh, in_specs=in_specs, out_specs=out_specs, check_vma=False)
```

profile of v0, /device:TPU:513, one launch (start us, length us, event | category | flops | bytes accessed | tf_op | source)
XLA Modules:
  0.0 445.0 jit_solution(16208365447369900026)
XLA Ops:
  6.6 0.7 compare_select_fusion
  7.2 0.7 compare_and_fusion
  7.9 1.7 copy.5
  10.0 0.6 gather_fusion
  10.6 1.2 select_bitcast_fusion
  11.9 1.7 copy.7
  13.6 4.5 %convolution_multiply_fusion = f32[640,640]{0,1:T(8,128)} fusion(f32[512,640]{0,1:T(8,128)S(1)} %bitcast.79), kind=kOutput, calls=%fused_computation.9 | convolution fusion | flops 2516992000 | bytes 2949120 | tf_op jit(solution)/shard_map/dot_general | solution.py:11
  18.1 0.9 iota_compare_fusion
  19.0 1.3 fusion.20
  20.3 212.0 %all-reduce.3.cloned.1.call-done = f32[640,640]{0,1:T(8,128)} async-done(((f32[640,640]{0,1:T(8,128)}), f32[640,640]{0,1:T(8,128)}) %all-reduce.3.cloned.1.call-update) | async-done | bytes 1638416 | tf_op jit(solution)/shard_map/psum | solution.py:35
  232.3 3.3 copy.9
  235.6 1.6 fusion
  237.2 1.2 copy-done.1
  238.4 11.7 %cholesky.133 = f32[128,128]{1,0:T(8,128)S(1)} custom-call(f32[128,128]{1,0:T(8,128)S(1)} %cholesky.340), custom_call_target="Cholesky" | custom-call | tf_op jit(solution)/shard_map/jit(cholesky)/cholesky | solution.py:25
  250.2 9.8 %custom-call.38 = f32[1,128,128]{1,2,0:T(8,128)S(1)} custom-call(f32[1,128,128]{2,1,0:T(8,128)S(1)} %get-tuple-element.35), custom_call_target="InvertDiagBlocksLowerTriangular" | custom-call | tf_op jit(solution)/shard_map/jit(cholesky)/cholesky | solution.py:25
  260.1 1.3 constant_dynamic-update-slice_fusion.8
  261.4 1.3 convolution_subtract_fusion.3
  262.8 11.7 %cholesky.272 = f32[128,128]{1,0:T(8,128)S(1)} custom-call(f32[128,128]{1,0:T(8,128)S(1)} %cholesky.344), custom_call_target="Cholesky" | custom-call | tf_op jit(solution)/shard_map/jit(cholesky)/cholesky | solution.py:25
  274.5 10.0 %custom-call.39 = f32[1,128,128]{1,2,0:T(8,128)S(1)} custom-call(f32[1,128,128]{2,1,0:T(8,128)S(1)} %get-tuple-element.32), custom_call_target="InvertDiagBlocksLowerTriangular" | custom-call | tf_op jit(solution)/shard_map/jit(cholesky)/cholesky | solution.py:25
  284.8 1.4 convolution_subtract_fusion.4
  286.2 11.7 %cholesky.293 = f32[128,128]{1,0:T(8,128)S(1)} custom-call(f32[128,128]{1,0:T(8,128)S(1)} %cholesky.349), custom_call_target="Cholesky" | custom-call | tf_op jit(solution)/shard_map/jit(cholesky)/cholesky | solution.py:25
  298.0 0.6 compare_reduce_fusion.2
  298.6 9.8 %custom-call.40 = f32[1,128,128]{1,2,0:T(8,128)S(1)} custom-call(f32[1,128,128]{2,1,0:T(8,128)S(1)} %get-tuple-element.29), custom_call_target="InvertDiagBlocksLowerTriangular" | custom-call | tf_op jit(solution)/shard_map/jit(cholesky)/cholesky | solution.py:25
  308.7 1.4 convolution_subtract_fusion.5
  310.1 11.9 %cholesky.312 = f32[128,128]{1,0:T(8,128)S(1)} custom-call(f32[128,128]{1,0:T(8,128)S(1)} %cholesky.354), custom_call_target="Cholesky" | custom-call | tf_op jit(solution)/shard_map/jit(cholesky)/cholesky | solution.py:25
  322.0 0.7 compare_reduce_fusion.1
  322.7 9.8 %custom-call.41 = f32[1,128,128]{1,2,0:T(8,128)S(1)} custom-call(f32[1,128,128]{2,1,0:T(8,128)S(1)} %get-tuple-element.26), custom_call_target="InvertDiagBlocksLowerTriangular" | custom-call | tf_op jit(solution)/shard_map/jit(cholesky)/cholesky | solution.py:25
  332.7 1.2 convolution_subtract_fusion.6
  334.0 11.7 %cholesky.329 = f32[128,128]{1,0:T(8,128)S(1)} custom-call(f32[128,128]{1,0:T(8,128)S(1)} %convolution_subtract_fusion.6), custom_call_target="Cholesky" | custom-call | tf_op jit(solution)/shard_map/jit(cholesky)/cholesky | solution.py:25
  345.7 0.7 compare_reduce_fusion
  346.4 0.7 compare_reduce_fusion.3
  350.1 1.3 select_select_fusion
  351.4 17.1 %while.1 = (s32[]{:T(128)}, f32[640,640]{1,0:T(8,128)}, s32[5,2]{0,1:T(2,128)S(1)}, f32[5,128,128]{2,1,0:T(8,128)}, s32[]{:T(128)}) while((s32[]{:T(128)}, f32[640,640]{1,0:T(8,128)}, s32[5,2]{0,1:T(2,128)S(1)}, f32[5,128,128]{2,1,0:T(8,128)}, s32[]{:T(128)}) %tuple.33), condition=%wide.while_cond, body=%wide.while_body.sunk | while | flops 2 | bytes 132705 | solution.py:26
  351.5 0.5 fusion.60
  352.0 2.8 bitcast_dynamic-update-slice_fusion.2
  355.5 2.8 bitcast_dynamic-update-slice_fusion.2
  358.9 2.8 bitcast_dynamic-update-slice_fusion.2
  362.3 2.8 bitcast_dynamic-update-slice_fusion.2
  365.8 2.7 bitcast_dynamic-update-slice_fusion.2
  368.5 50.3 %custom-call.42 = f32[5,128,128]{1,2,0:T(8,128)S(1)} custom-call(f32[5,128,128]{2,1,0:T(8,128)} %get-tuple-element.12), custom_call_target="InvertDiagBlocksLowerTriangular" | custom-call | tf_op jit(solution)/shard_map/triangular_solve | solution.py:26
  418.8 1.1 constant_dynamic-update-slice_fusion.3
  420.0 1.4 convolution_subtract_fusion.1
  421.9 1.4 convolution_subtract_fusion
  423.8 1.8 convolution_subtract_fusion.2
  426.1 1.9 fusion.9
  428.4 6.4 %convolution_bitcast_fusion = f32[5,512,128]{2,1,0:T(8,128)S(1)} fusion(f32[512,640,1]{0,1,2:T(8,128)S(1)} %bitcast.80, f32[5,128,640]{2,1,0:T(8,128)S(1)} %bitcast.83), kind=kOutput, calls=%fused_computation.10 | convolution fusion | flops 2516582400 | bytes 4259840 | tf_op jit(solution)/shard_map/dot_general | solution.py:21
  434.9 0.9 scatter_fusion
  436.2 1.5 copy.12
  (40 shorter events, 6.4 us)
Async XLA Ops:
  6.5 225.8 %all-reduce.3.cloned.1.call-start = ((), (), s32[]{:S(2)}) async-start(), calls=%async_computation | async-start | bytes 3276800 | tf_op jit(solution)/shard_map/psum | solution.py:35
  232.3 3.3 copy-start
  237.2 1.2 copy-start.1
  368.5 53.4 %copy-start.2 = (f32[640,640]{1,0:T(8,128)S(1)}, f32[640,640]{1,0:T(8,128)}, u32[]{:S(2)}) copy-start(f32[640,640]{1,0:T(8,128)} %fusion.20) | copy-start | bytes 4915204
Sparse Core Ops, SparseCore 0:
  18.2 214.0 all-reduce.2
where the time goes:
time: 450 us; the launch traced here: 445 us
  waiting for transfers between devices  212 us (47%)
  other arithmetic  159 us (35%)
  local copies, waits for them, and re-layouts  29 us (6%)
  matrix products  27.8 us (6%)
  between operations  17.2 us (4%)
    psum x1, waiting for transfers between devices, local(): whole = lax.psum(contract(reordered, reordered) * scale, 'grid')  212 us
    another operation x18, other arithmetic, factor_inverse(): lower = jnp.linalg.cholesky(gram)  101 us
    another operation x3, other arithmetic, factor_inverse(): lax.linalg.triangular_solve(lower, jnp.eye(width, dtype=gram.dtype), left...  51.6 us
    another operation x15, local copies, waits for them, and re-layouts  17.1 us
    another operation x9, matrix products, factor_inverse(): lax.linalg.triangular_solve(lower, jnp.eye(width, dtype=gram.dtype), left...  9.55 us
  transfers between devices with their start and end apart: 1, of which 1 were waited for; matrix products, arithmetic and copies ran while one was open for 0% of the time, Pallas kernels for 0%

commit v1 on v0

v1 whole, which is shorter than its diff:
```python
import jax
import jax.numpy as jnp
from jax import lax
from jax.experimental import pallas as pl
from jax.experimental.pallas import tpu as pltpu
from jax.sharding import PartitionSpec as P

BLOCK = 128
NBLK = 5
PANEL = 16
PAIRS = [(i, j) for i in range(NBLK) for j in range(i, NBLK)]
SLOTS = 16
HIGHEST = lax.Precision.HIGHEST


def dot(left, right, contract):
    return lax.dot_general(
        left, right, (contract, ((), ())), precision=HIGHEST, preferred_element_type=jnp.float32
    )


def cols(ref, block):
    return ref[:, pl.ds(pl.multiple_of(block * BLOCK, BLOCK), BLOCK)]


def gram_kernel(scale, order_ref, psi_ref, out_ref, perm_ref):
    for i in range(NBLK):
        perm_ref[:, i * BLOCK:(i + 1) * BLOCK] = cols(psi_ref, order_ref[i])
    slot = 0
    for i in range(NBLK):
        row = dot(perm_ref[:, i * BLOCK:(i + 1) * BLOCK], perm_ref[:, i * BLOCK:], ((0,), (0,))) * scale
        for j in range(NBLK - i):
            out_ref[slot] = row[:, j * BLOCK:(j + 1) * BLOCK]
            slot += 1
    for extra in range(slot, SLOTS):
        out_ref[extra] = jnp.zeros((BLOCK, BLOCK), jnp.float32)


def factor_block(work_ref):
    row = lax.broadcasted_iota(jnp.int32, (PANEL, BLOCK), 0)
    for p in range(BLOCK // PANEL):
        r0 = p * PANEL
        part_a = work_ref[r0:r0 + PANEL, :BLOCK]
        part_e = work_ref[r0:r0 + PANEL, BLOCK:]
        columns = [
            jnp.broadcast_to(part_a[:, r0 + m:r0 + m + 1], (PANEL, BLOCK)) for m in range(PANEL)
        ]
        diag = jnp.ones((PANEL, BLOCK), jnp.float32)
        for k in range(PANEL):
            column = columns[k]
            pivot = column[k:k + 1, :]
            diag = jnp.where(row == k, pivot, diag)
            if k == PANEL - 1:
                break
            factor = jnp.where(row > k, column * (1.0 / pivot), 0.0)
            for m in range(k + 1, PANEL):
                columns[m] = columns[m] - factor * column[m:m + 1, :]
            part_a = part_a - factor * part_a[k:k + 1, :]
            part_e = part_e - factor * part_e[k:k + 1, :]
        norm = lax.rsqrt(diag)
        part_a = part_a * norm
        part_e = part_e * norm
        work_ref[r0:r0 + PANEL, BLOCK:] = part_e
        low = r0 + PANEL
        if low < BLOCK:
            both = jnp.concatenate([part_a, part_e], axis=1)
            update = dot(part_a, both, ((0,), (0,)))
            work_ref[low:, :] = work_ref[low:, :] - update[low:, :]
    return work_ref[:, BLOCK:]


def factor_kernel(core_ref, mine_ref, other_ref, out_ref, grid_ref, work_ref):
    core = core_ref[0]
    half = SLOTS // 2
    for slot, (i, j) in enumerate(PAIRS):
        own = (core == slot // half)
        value = jnp.where(own, mine_ref[slot % half], other_ref[slot % half])
        grid_ref[i, :, j * BLOCK:(j + 1) * BLOCK] = value
    for i in range(1, NBLK):
        grid_ref[i, :, :i * BLOCK] = jnp.zeros((BLOCK, i * BLOCK), jnp.float32)
    eye = (
        lax.broadcasted_iota(jnp.int32, (BLOCK, BLOCK), 0)
        == lax.broadcasted_iota(jnp.int32, (BLOCK, BLOCK), 1)
    ).astype(jnp.float32)
    for k in range(NBLK):
        here = slice(k * BLOCK, (k + 1) * BLOCK)
        after = slice((k + 1) * BLOCK, NBLK * BLOCK)
        work_ref[:, :BLOCK] = grid_ref[k, :, here]
        work_ref[:, BLOCK:] = eye
        inverse = factor_block(work_ref)
        grid_ref[k, :, here] = inverse
        if k + 1 < NBLK:
            right = dot(inverse, grid_ref[k, :, after], ((1,), (0,)))
            grid_ref[k, :, after] = right
        if k > 0:
            grid_ref[k, :, :k * BLOCK] = dot(inverse, grid_ref[k, :, :k * BLOCK], ((1,), (0,)))
        for i in range(k + 1, NBLK):
            lead = grid_ref[k, :, i * BLOCK:(i + 1) * BLOCK]
            grid_ref[i, :, i * BLOCK:] = grid_ref[i, :, i * BLOCK:] - dot(
                lead, grid_ref[k, :, i * BLOCK:], ((0,), (0,))
            )
            grid_ref[i, :, :(k + 1) * BLOCK] = grid_ref[i, :, :(k + 1) * BLOCK] - dot(
                lead, grid_ref[k, :, :(k + 1) * BLOCK], ((0,), (0,))
            )
    out_ref[...] = jnp.zeros(out_ref.shape, jnp.float32)
    for i in range(NBLK):
        for j in range(i + 1):
            out_ref[j * BLOCK:(j + 1) * BLOCK, i * BLOCK:(i + 1) * BLOCK] = (
                grid_ref[i, :, j * BLOCK:(j + 1) * BLOCK].T
            )


def apply_kernel(order_ref, psi_ref, inv_ref, out_ref, perm_ref):
    for i in range(NBLK):
        perm_ref[:, i * BLOCK:(i + 1) * BLOCK] = cols(psi_ref, order_ref[i])
    for first in range(0, NBLK, 2):
        last = min(first + 2, NBLK)
        value = dot(
            perm_ref[:, :last * BLOCK],
            inv_ref[:last * BLOCK, first * BLOCK:last * BLOCK],
            ((1,), (0,)),
        )
        for b in range(first, last):
            start = pl.multiple_of(order_ref[b] * BLOCK, BLOCK)
            out_ref[:, pl.ds(start, BLOCK)] = value[:, (b - first) * BLOCK:(b - first + 1) * BLOCK]


def vmem():
    return pl.BlockSpec(memory_space=pltpu.VMEM)


def smem():
    return pl.BlockSpec(memory_space=pltpu.SMEM)


def local(psi, order):
    rows, bands = psi.shape
    size = lax.axis_size("grid")
    chips = size // 2
    scale = 1.0 / (rows * size)
    index = lax.axis_index("grid")
    core = index % 2
    pairs = [(d, d ^ 1) for d in range(size)]
    groups = [list(range(c, size, 2)) for c in range(2)]
    half = SLOTS // 2
    chunk = half * BLOCK // chips

    gram = pl.pallas_call(
        lambda *refs: gram_kernel(scale, *refs),
        out_shape=jax.ShapeDtypeStruct((SLOTS, BLOCK, BLOCK), jnp.float32),
        in_specs=[smem(), vmem()],
        out_specs=vmem(),
        scratch_shapes=[pltpu.VMEM((rows, bands), jnp.float32)],
        name="gram",
    )(order, psi)

    gram = gram.reshape(2, half, BLOCK, BLOCK)
    keep = lax.dynamic_index_in_dim(gram, core, 0, keepdims=False)
    send = lax.dynamic_index_in_dim(gram, 1 - core, 0, keepdims=False)
    both = keep + lax.ppermute(send, "grid", pairs)
    parts = lax.all_to_all(
        both.reshape(chips, chunk, BLOCK), "grid", 0, 0, axis_index_groups=groups, tiled=True
    )
    total = jnp.sum(parts, axis=0)
    mine = lax.all_to_all(
        jnp.broadcast_to(total[None], parts.shape), "grid", 0, 0, axis_index_groups=groups, tiled=True
    ).reshape(half, BLOCK, BLOCK)
    other = lax.ppermute(mine, "grid", pairs)

    inverse = pl.pallas_call(
        factor_kernel,
        out_shape=jax.ShapeDtypeStruct((bands, bands), jnp.float32),
        in_specs=[smem(), vmem(), vmem()],
        out_specs=vmem(),
        scratch_shapes=[
            pltpu.VMEM((NBLK, BLOCK, bands), jnp.float32),
            pltpu.VMEM((BLOCK, 2 * BLOCK), jnp.float32),
        ],
        name="factor",
    )(core.astype(jnp.int32).reshape(1), mine, other)

    return pl.pallas_call(
        apply_kernel,
        out_shape=jax.ShapeDtypeStruct((rows, bands), jnp.float32),
        in_specs=[smem(), vmem(), vmem()],
        out_specs=vmem(),
        scratch_shapes=[pltpu.VMEM((rows, bands), jnp.float32)],
        name="apply",
    )(order, psi, inverse)


def solution(mesh):
    in_specs = (P(("frag", "grid"), None), P("frag"))
    out_specs = P(("frag", "grid"), None)
    return jax.shard_map(local, mesh=mesh, in_specs=in_specs, out_specs=out_specs, check_vma=False)
```

time: 450 us -> 115 us (0.26); the launches traced: 445 us -> 115 us
  waiting for transfers between devices: 212 us -> 3.07 us
  other arithmetic: 159 us -> 0.13 us
  blocking collectives: 0 us -> 45.4 us
  Pallas kernels: 0 us -> 39.5 us
  matrix products: 27.8 us -> 0 us
  local copies, waits for them, and re-layouts: 29 us -> 2.01 us
  starting transfers between devices: 0.01 us -> 24.4 us
  between operations: 17.2 us -> 0.03 us
    psum x1 -> x0, waiting for transfers between devices: 212 us -> none  [local(): whole = lax.psum(contract(reordered, reordered) * scale, 'grid')]
    another operation x21 -> x0, other arithmetic: 153 us -> none  [the longest x18 101 us: factor_inverse(): lower = jnp.linalg.cholesky(gram)]
    all_to_all x0 -> x2, blocking collectives: none -> 45.4 us  [the longest x1 23 us: local(): lax.all_to_all(jnp.broadcast_to(total[None], parts.shape), 'grid', 0, 0,...]
    pallas_call x0 -> x3, Pallas kernels: none -> 39.5 us  [the longest x1 29.6 us: local(): pl.pallas_call(factor_kernel, out_shape=jax.ShapeDtypeStruct((bands, band...]
    ppermute x0 -> x2, starting transfers between devices: none -> 24.4 us  [the longest x1 20.5 us: local(): both = keep + lax.ppermute(send, 'grid', pairs)]
    another operation x21 -> x0, local copies, waits for them, and re-layouts: 17.2 us -> none
    another operation x17 -> x0, matrix products: 17 us -> none  [the longest x9 9.55 us: factor_inverse(): lax.linalg.triangular_solve(lower, jnp.eye(width, dtype=gram.dtype), left...]
    dot_general x2 -> x0, matrix products: 10.8 us -> none  [the longest x1 6.36 us: matmul(): jnp.dot(left, right, precision=lax.Precision.HIGHEST, preferred_element_t...]
  transfers between devices with their start and end apart: 1 -> 2, of which waited for: 1 -> 2; matrix products, arithmetic and copies ran while one was open for 0% -> 0% of each run, Pallas kernels for 0% -> 0%
where the time goes in v1:
time: 115 us
  blocking collectives  45.4 us (39%)
  Pallas kernels  39.5 us (34%)
  starting transfers between devices  24.4 us (21%)
  waiting for transfers between devices  3.07 us (3%)
  local copies, waits for them, and re-layouts  2.01 us (2%)
    pallas_call x1, Pallas kernels, local(): pl.pallas_call(factor_kernel, out_shape=jax.ShapeDtypeStruct((bands, band...  29.6 us
    all_to_all x1, blocking collectives, local(): lax.all_to_all(jnp.broadcast_to(total[None], parts.shape), 'grid', 0, 0,...  23 us
    all_to_all x1, blocking collectives, local(): lax.all_to_all(both.reshape(chips, chunk, BLOCK), 'grid', 0, 0, axis_inde...  22.4 us
    ppermute x1, starting transfers between devices, local(): both = keep + lax.ppermute(send, 'grid', pairs)  20.5 us
    pallas_call x1, Pallas kernels, local(): pl.pallas_call(apply_kernel, out_shape=jax.ShapeDtypeStruct((rows, bands)...  5.4 us
    pallas_call x1, Pallas kernels, local(): pl.pallas_call(lambda *refs: gram_kernel(scale, *refs), out_shape=jax.Sha...  4.5 us
    ppermute x1, starting transfers between devices, local(): other = lax.ppermute(mine, 'grid', pairs)  3.89 us
  transfers between devices with their start and end apart: 2, of which 2 were waited for; matrix products, arithmetic and copies ran while one was open for 0% of the time, Pallas kernels for 0%

profile of v1, /device:TPU:513, one launch (start us, length us, event | category | flops | bytes accessed | tf_op | source)
XLA Modules:
  0.0 114.6 jit_solution(452805520946388536)
XLA Ops:
  0.0 4.5 %gram.1 = f32[16,128,128]{2,1,0:T(8,128)} custom-call(s32[5]{0:T(128)} %order_ref.1, f32[512,640]{1,0:T(8,128)} %psi_ref.1), custom_call_target="tpu_custom_call" | custom-call | tf_op jit(solution)/shard_map/gram/pallas_call | solution.py:148
  4.5 0.0 copy-start
  4.5 1.2 %dynamic-slice_bitcast_fusion = f32[8,128,128]{2,1,0:T(8,128)S(1)} fusion(f32[2,8,128,128]{3,2,1,0:T(8,128)} %bitcast.8, s32[]{:T(128)S(6)} %select_n.16), kind=kLoop, calls=%fused_computation.1 | loop fusion | bytes 1048580 | tf_op jit(solution)/shard_map/jit(dynamic_index_in_dim)/squeeze | solution.py:159
  5.7 20.5 %collective-permute-start = (f32[8,128,128]{2,1,0:T(8,128)S(1)}, f32[8,128,128]{2,1,0:T(8,128)S(1)}, u32[]{:S(2)}, u32[]{:S(2)}) collective-permute-start(f32[8,128,128]{2,1,0:T(8,128)S(1)} %dynamic-slice_bitcast_fusion), channel_id=1, source_target_pairs={{0,1},{1,0},{2,3},{3,2},{4,5},{5,4},{6,7},{7,6},{8,9},{9,8},{10,11... | collective-permute-start | bytes 1572872 | tf_op jit(solution)/shard_map/ppermute | solution.py:160
  26.2 1.5 %collective-permute-done = f32[8,128,128]{2,1,0:T(8,128)S(1)} collective-permute-done((f32[8,128,128]{2,1,0:T(8,128)S(1)}, f32[8,128,128]{2,1,0:T(8,128)S(1)}, u32[]{:S(2)}, u32[]{:S(2)}) %collective-permute-start) | collective-permute-done | bytes 524320 | tf_op jit(solution)/shard_map/ppermute | solution.py:160
  27.7 0.0 copy-done
  27.7 0.1 bitcast_add_fusion
  27.8 22.4 %all_to_all.10 = f32[64,16,128]{2,1,0:T(8,128)S(1)} all-to-all(f32[64,16,128]{2,1,0:T(8,128)S(1)} %bitcast.10), channel_id=1, replica_groups={{0,2,4,6,8,10,12,14,16,18,20,22,24,26,28,30,32,34,36,38,40,42,44,46,48,..., dimensions={0} | all-to-all | bytes 1048576 | tf_op jit(solution)/shard_map/all_to_all | solution.py:161
  50.2 0.1 reduce_sum.9
  50.3 23.0 %all_to_all.11 = f32[64,16,128]{2,1,0:T(8,128)S(1)} all-to-all(f32[64,16,128]{2,1,0:T(8,128)S(1)} %broadcast_in_dim.2), channel_id=1, replica_groups={{0,2,4,6,8,10,12,14,16,18,20,22,24,26,28,30,32,34,36,38,40,42,44,46,48,..., dimensions={0} | all-to-all | bytes 1048576 | tf_op jit(solution)/shard_map/all_to_all | solution.py:165
  73.4 0.0 copy-start.1
  73.4 3.9 %collective-permute-start.1 = (f32[8,128,128]{2,1,0:T(8,128)S(1)}, f32[8,128,128]{2,1,0:T(8,128)S(1)}, u32[]{:S(2)}, u32[]{:S(2)}) collective-permute-start(f32[8,128,128]{2,1,0:T(8,128)S(1)} %bitcast.11), channel_id=1, source_target_pairs={{0,1},{1,0},{2,3},{3,2},{4,5},{5,4},{6,7},{7,6},{8,9},{9,8},{10,11... | collective-permute-start | bytes 1572872 | tf_op jit(solution)/shard_map/ppermute | solution.py:168
  77.2 1.5 %collective-permute-done.1.other_ref = f32[8,128,128]{2,1,0:T(8,128)S(1)} collective-permute-done((f32[8,128,128]{2,1,0:T(8,128)S(1)}, f32[8,128,128]{2,1,0:T(8,128)S(1)}, u32[]{:S(2)}, u32[]{:S(2)}) %collective-permute-start.1) | collective-permute-done | bytes 524320 | tf_op jit(solution)/shard_map/ppermute | solution.py:168
  78.8 0.0 copy-start.2
  78.8 0.0 copy-done.1
  78.8 0.8 copy-done.2
  79.6 29.6 %factor.1.inv_ref = f32[640,640]{1,0:T(8,128)} custom-call(s32[1]{0:T(128)} %bitcast.core_ref, f32[8,128,128]{2,1,0:T(8,128)} %bitcast.12, f32[8,128,128]{2,1,0:T(8,128)} %copy-done.2), custom_call_target="tpu_custom_call" | custom-call | tf_op jit(solution)/shard_map/factor/pallas_call | solution.py:170
  109.2 5.4 %apply.1 = f32[512,640]{1,0:T(8,128)} custom-call(s32[5]{0:T(128)} %order_ref.1, f32[512,640]{1,0:T(8,128)} %psi_ref.1, f32[640,640]{1,0:T(8,128)} %factor.1.inv_ref), custom_call_target="tpu_custom_call" | custom-call | tf_op jit(solution)/shard_map/apply/pallas_call | solution.py:182
  (1 shorter events, 0.0 us)
Async XLA Ops:
  4.5 23.2 %copy-start = (f32[16,128,128]{2,1,0:T(8,128)S(1)}, f32[16,128,128]{2,1,0:T(8,128)}, u32[]{:S(2)}) copy-start(f32[16,128,128]{2,1,0:T(8,128)} %gram.1) | copy-start | bytes 3145732
  5.7 22.1 %collective-permute-start = (f32[8,128,128]{2,1,0:T(8,128)S(1)}, f32[8,128,128]{2,1,0:T(8,128)S(1)}, u32[]{:S(2)}, u32[]{:S(2)}) collective-permute-start(f32[8,128,128]{2,1,0:T(8,128)S(1)} %dynamic-slice_bitcast_fusion), channel_id=1, source_target_pairs={{0,1},{1,0},{2,3},{3,2},{4,5},{5,4},{6,7},{7,6},{8,9},{9,8},{10,11... | collective-permute-start | bytes 1572872 | tf_op jit(solution)/shard_map/ppermute | solution.py:160
  73.4 5.4 %copy-start.1 = (f32[64,16,128]{2,1,0:T(8,128)}, f32[64,16,128]{2,1,0:T(8,128)S(1)}, u32[]{:S(2)}) copy-start(f32[64,16,128]{2,1,0:T(8,128)S(1)} %all_to_all.11) | copy-start | bytes 1572868
  73.4 5.4 %collective-permute-start.1 = (f32[8,128,128]{2,1,0:T(8,128)S(1)}, f32[8,128,128]{2,1,0:T(8,128)S(1)}, u32[]{:S(2)}, u32[]{:S(2)}) collective-permute-start(f32[8,128,128]{2,1,0:T(8,128)S(1)} %bitcast.11), channel_id=1, source_target_pairs={{0,1},{1,0},{2,3},{3,2},{4,5},{5,4},{6,7},{7,6},{8,9},{9,8},{10,11... | collective-permute-start | bytes 1572872 | tf_op jit(solution)/shard_map/ppermute | solution.py:168
  78.8 0.8 copy-start.2

commit v2 on v0

v2 whole, which is shorter than its diff:
```python
import jax
import jax.numpy as jnp
from jax import lax
from jax.experimental import pallas as pl
from jax.experimental.pallas import tpu as pltpu
from jax.sharding import PartitionSpec as P

BLOCK = 128
NBLK = 5
PANEL = 32
SUB = 8
PAIRS = [(i, j) for i in range(NBLK) for j in range(i, NBLK)]
SLOT = {pair: slot for slot, pair in enumerate(PAIRS)}
SLOTS = 16
HIGHEST = lax.Precision.HIGHEST


def dot(left, right):
    return lax.dot_general(
        left, right, (((1,), (0,)), ((), ())), precision=HIGHEST, preferred_element_type=jnp.float32
    )


def dot_tn(left, right):
    return lax.dot_general(
        left, right, (((0,), (0,)), ((), ())), precision=HIGHEST, preferred_element_type=jnp.float32
    )


def dot_nt(left, right):
    return lax.dot_general(
        left, right, (((1,), (1,)), ((), ())), precision=HIGHEST, preferred_element_type=jnp.float32
    )


def span(first, last):
    return slice(first * BLOCK, last * BLOCK)


def block_copies(order_ref, far_ref, near_ref, sems, outward=False):
    copies = []
    for b in range(NBLK):
        start = pl.multiple_of(order_ref[b] * BLOCK, BLOCK)
        far = far_ref.at[:, pl.ds(start, BLOCK)]
        near = near_ref.at[:, span(b, b + 1)]
        copies.append(
            pltpu.make_async_copy(near, far, sems.at[b])
            if outward
            else pltpu.make_async_copy(far, near, sems.at[b])
        )
    return copies


def gram_kernel(scale, order_ref, psi_ref, out_ref, x_ref, sems):
    loads = block_copies(order_ref, psi_ref, x_ref, sems)
    for load in loads:
        load.start()
    for load in loads:
        load.wait()
    for i in range(NBLK):
        row = dot_tn(x_ref[:, span(i, i + 1)], x_ref[:, i * BLOCK:]) * scale
        for j in range(i, NBLK):
            out_ref[SLOT[i, j]] = row[:, span(j - i, j - i + 1)]
    for extra in range(len(PAIRS), SLOTS):
        out_ref[extra] = jnp.zeros((BLOCK, BLOCK), jnp.float32)


def eliminate(work_ref, col_ref, between):
    lane = lax.broadcasted_iota(jnp.int32, (SUB, BLOCK), 1)
    row = lax.broadcasted_iota(jnp.int32, (SUB, BLOCK), 0)
    pieces = PANEL // SUB
    for p in range(BLOCK // PANEL):
        r0 = p * PANEL
        low = r0 + PANEL
        for m in range(PANEL):
            top = m // SUB * SUB
            col_ref[m, top:, :] = jnp.broadcast_to(
                work_ref[r0 + top:low, r0 + m:r0 + m + 1], (PANEL - top, BLOCK)
            )
        inside = (lane >= r0) & (lane < low)
        part = []
        for q in range(pieces):
            unit = (lane == row + (r0 + q * SUB)).astype(jnp.float32)
            part.append(jnp.where(inside, unit, work_ref[r0 + q * SUB:r0 + (q + 1) * SUB, :]))
        column = {
            (m, q): col_ref[m, q * SUB:(q + 1) * SUB, :]
            for m in range(PANEL)
            for q in range(m // SUB, pieces)
        }
        diag = [jnp.ones((SUB, BLOCK), jnp.float32)] * pieces
        for k in range(PANEL):
            kq, ks = divmod(k, SUB)
            pivot = column[k, kq][ks:ks + 1, :]
            inverse = 1.0 / pivot
            diag[kq] = jnp.where(row == ks, pivot, diag[kq])
            factor = {q: column[k, q] * inverse for q in range(kq, pieces)}
            for m in range(k + 1, PANEL):
                mq, ms = divmod(m, SUB)
                entry = column[k, mq][ms:ms + 1, :]
                for q in range(mq, pieces):
                    column[m, q] = column[m, q] - factor[q] * entry
            lead = part[kq][ks:ks + 1, :]
            part[kq] = part[kq] - jnp.where(row > ks, factor[kq], 0.0) * lead
            for q in range(kq + 1, pieces):
                part[q] = part[q] - factor[q] * lead
        whole = jnp.concatenate([part[q] * lax.rsqrt(diag[q]) for q in range(pieces)], axis=0)
        work_ref[r0:low, :] = whole
        if low < BLOCK:
            update = dot(whole.T[low:, :], whole)
            rest = lax.broadcasted_iota(jnp.int32, (BLOCK - low, BLOCK), 1)
            kept = jnp.where((rest >= r0) & (rest < low), 0.0, work_ref[low:, :])
            work_ref[low:, :] = kept - update
        between()


def finish_kernel(
    core_ref, order_ref, mine_ref, other_ref, psi_ref, out_ref,
    a_ref, inv_ref, pair_ref, x_ref, q_ref, work_ref, col_ref, in_sems, out_sems,
):
    loads = block_copies(order_ref, psi_ref, x_ref, in_sems)
    stores = block_copies(order_ref, out_ref, q_ref, out_sems, outward=True)
    for load in loads:
        load.start()
    core = core_ref[0]
    half = SLOTS // 2
    for slot, (i, j) in enumerate(PAIRS):
        own = core == slot // half
        a_ref[span(i, i + 1), span(j, j + 1)] = jnp.where(
            own, mine_ref[slot % half], other_ref[slot % half]
        )
    lower = (
        lax.broadcasted_iota(jnp.int32, (BLOCK, BLOCK), 0)
        >= lax.broadcasted_iota(jnp.int32, (BLOCK, BLOCK), 1)
    )
    rows = x_ref.shape[0]
    tiles = [slice(r, r + BLOCK) for r in range(0, rows, BLOCK)]
    soon, whenever = [], []

    def a(i, j, wide=1):
        return a_ref[span(i, i + 1), span(j, j + wide)]

    def solve(k, j, wide=1):
        a_ref[span(k, k + 1), span(j, j + wide)] = dot(inv_ref[k], a(k, j, wide))

    def downdate(i, j, first, last, wide=1):
        ks = span(first, last)
        a_ref[span(i, i + 1), span(j, j + wide)] = a(i, j, wide) - dot_tn(
            a_ref[ks, span(i, i + 1)], a_ref[ks, span(j, j + wide)]
        )

    def couple(k):
        pair_ref[k, BLOCK:, :BLOCK] = dot_tn(a(k, k + 1), inv_ref[k])

    def pair(k):
        pair_ref[k, :BLOCK, :BLOCK] = inv_ref[k]
        pair_ref[k, BLOCK:, BLOCK:] = inv_ref[k + 1]
        pair_ref[k, :BLOCK, BLOCK:] = jnp.zeros((BLOCK, BLOCK), jnp.float32)
        pair_ref[k, BLOCK:, :BLOCK] = -dot(inv_ref[k + 1], pair_ref[k, BLOCK:, :BLOCK])

    def finish(k, wide, tile):
        factor = pair_ref[k] if wide == 2 else inv_ref[k]
        q_ref[tile, span(k, k + wide)] = dot_nt(x_ref[tile, span(k, k + wide)], factor)

    def project(first, last, tile):
        x_ref[tile, last * BLOCK:] = x_ref[tile, last * BLOCK:] - dot(
            q_ref[tile, span(first, last)], a_ref[span(first, last), last * BLOCK:]
        )

    def send(first, last):
        for b in range(first, last):
            stores[b].start()

    def after(k):
        if k + 1 == NBLK:
            return
        solve(k, k + 1)
        downdate(k + 1, k + 1, k, k + 1)
        first = k // 2 * 2
        if k % 2 == 0:
            soon.append(lambda: couple(k))
            if k + 2 < NBLK:
                soon.append(lambda: solve(k, k + 2))
                soon.append(lambda: downdate(k + 1, k + 2, k, k + 1))
                soon.append(lambda: downdate(k + 2, k + 2, k, k + 1))
            if k + 3 < NBLK:
                soon.append(lambda: solve(k, k + 3, NBLK - k - 3))
                soon.append(lambda: downdate(k + 1, k + 3, k, k + 1, NBLK - k - 3))
        else:
            if k + 2 < NBLK:
                soon.append(lambda: solve(k, k + 2, NBLK - k - 2))
                soon.append(lambda: downdate(k + 1, k + 2, first, k + 1, NBLK - k - 2))
                for i in range(k + 2, NBLK):
                    soon.append(lambda i=i: downdate(i, i, first, k + 1, NBLK - i))
            whenever.append(lambda: pair(first))
            for tile in tiles:
                whenever.append(lambda tile=tile: finish(first, 2, tile))
            whenever.append(lambda: send(first, k + 1))
            for tile in tiles:
                whenever.append(lambda tile=tile: project(first, k + 1, tile))

    def run(queue, count):
        for _ in range(min(count, len(queue))):
            queue.pop(0)()

    panels = BLOCK // PANEL
    for k in range(NBLK):
        work_ref[...] = a(k, k)
        state = {"left": panels}

        def between():
            run(soon, -(-len(soon) // max(state["left"] - 1, 1)))
            more = panels if k % 2 == 0 and k + 1 < NBLK else 0
            turns = state["left"] + more
            run(whenever, -(-len(whenever) // turns))
            state["left"] -= 1

        eliminate(work_ref, col_ref, between)
        run(soon, len(soon))
        inv_ref[k] = jnp.where(lower, work_ref[...], 0.0)
        if k == 1:
            for load in loads:
                load.wait()
        after(k)
    run(whenever, len(whenever))
    last = NBLK - 1
    for tile in tiles:
        finish(last, 1, tile)
    send(last, NBLK)
    for store in stores:
        store.wait()


def vmem():
    return pl.BlockSpec(memory_space=pltpu.VMEM)


def smem():
    return pl.BlockSpec(memory_space=pltpu.SMEM)


def anywhere():
    return pl.BlockSpec(memory_space=pl.ANY)


def finish_scratch(rows):
    bands = NBLK * BLOCK
    return [
        pltpu.VMEM((bands, bands), jnp.float32),
        pltpu.VMEM((NBLK, BLOCK, BLOCK), jnp.float32),
        pltpu.VMEM((NBLK, 2 * BLOCK, 2 * BLOCK), jnp.float32),
        pltpu.VMEM((rows, bands), jnp.float32),
        pltpu.VMEM((rows, bands), jnp.float32),
        pltpu.VMEM((BLOCK, BLOCK), jnp.float32),
        pltpu.VMEM((PANEL, PANEL, BLOCK), jnp.float32),
        pltpu.SemaphoreType.DMA((NBLK,)),
        pltpu.SemaphoreType.DMA((NBLK,)),
    ]


def local(psi, order):
    rows, bands = psi.shape
    size = lax.axis_size("grid")
    chips = size // 2
    scale = 1.0 / (rows * size)
    core = lax.axis_index("grid") % 2
    pairs = [(d, d ^ 1) for d in range(size)]
    groups = [list(range(c, size, 2)) for c in range(2)]
    half = SLOTS // 2
    chunk = half * BLOCK // chips

    gram = pl.pallas_call(
        lambda *refs: gram_kernel(scale, *refs),
        out_shape=jax.ShapeDtypeStruct((SLOTS, BLOCK, BLOCK), jnp.float32),
        in_specs=[smem(), anywhere()],
        out_specs=vmem(),
        scratch_shapes=[
            pltpu.VMEM((rows, bands), jnp.float32),
            pltpu.SemaphoreType.DMA((NBLK,)),
        ],
        name="gram",
    )(order, psi)

    gram = gram.reshape(2, half, BLOCK, BLOCK)
    keep = lax.dynamic_index_in_dim(gram, core, 0, keepdims=False)
    send = lax.dynamic_index_in_dim(gram, 1 - core, 0, keepdims=False)
    both = keep + lax.ppermute(send, "grid", pairs)
    parts = lax.all_to_all(
        both.reshape(chips, chunk, BLOCK), "grid", 0, 0, axis_index_groups=groups, tiled=True
    )
    total = jnp.sum(parts, axis=0)
    mine = lax.all_to_all(
        jnp.broadcast_to(total[None], parts.shape), "grid", 0, 0, axis_index_groups=groups, tiled=True
    ).reshape(half, BLOCK, BLOCK)
    other = lax.ppermute(mine, "grid", pairs)

    return pl.pallas_call(
        finish_kernel,
        out_shape=jax.ShapeDtypeStruct((rows, bands), jnp.float32),
        in_specs=[smem(), smem(), vmem(), vmem(), anywhere()],
        out_specs=anywhere(),
        scratch_shapes=finish_scratch(rows),
        name="finish",
    )(core.astype(jnp.int32).reshape(1), order, mine, other, psi)


def solution(mesh):
    in_specs = (P(("frag", "grid"), None), P("frag"))
    out_specs = P(("frag", "grid"), None)
    return jax.shard_map(local, mesh=mesh, in_specs=in_specs, out_specs=out_specs, check_vma=False)
```

time: 450 us -> 101 us (0.22); the launches traced: 445 us -> 101 us
  waiting for transfers between devices: 212 us -> 3.07 us
  other arithmetic: 159 us -> 0.13 us
  blocking collectives: 0 us -> 45.4 us
  matrix products: 27.8 us -> 0 us
  local copies, waits for them, and re-layouts: 29 us -> 2.01 us
  Pallas kernels: 0 us -> 25.6 us
  starting transfers between devices: 0.01 us -> 24.4 us
  between operations: 17.2 us -> 0.22 us
    psum x1 -> x0, waiting for transfers between devices: 212 us -> none  [local(): whole = lax.psum(contract(reordered, reordered) * scale, 'grid')]
    another operation x21 -> x0, other arithmetic: 153 us -> none  [the longest x18 101 us: factor_inverse(): lower = jnp.linalg.cholesky(gram)]
    all_to_all x0 -> x2, blocking collectives: none -> 45.4 us  [the longest x1 23 us: local(): lax.all_to_all(jnp.broadcast_to(total[None], parts.shape), 'grid', 0, 0,...]
    pallas_call x0 -> x2, Pallas kernels: none -> 25.6 us  [the longest x1 20.3 us: local(): pl.pallas_call(finish_kernel, out_shape=jax.ShapeDtypeStruct((rows, bands...]
    ppermute x0 -> x2, starting transfers between devices: none -> 24.4 us  [the longest x1 20.5 us: local(): both = keep + lax.ppermute(send, 'grid', pairs)]
    another operation x21 -> x0, local copies, waits for them, and re-layouts: 17.2 us -> none
    another operation x17 -> x0, matrix products: 17 us -> none  [the longest x9 9.55 us: factor_inverse(): lax.linalg.triangular_solve(lower, jnp.eye(width, dtype=gram.dtype), left...]
    dot_general x2 -> x0, matrix products: 10.8 us -> none  [the longest x1 6.36 us: matmul(): jnp.dot(left, right, precision=lax.Precision.HIGHEST, preferred_element_t...]
  transfers between devices with their start and end apart: 1 -> 2, of which waited for: 1 -> 2; matrix products, arithmetic and copies ran while one was open for 0% -> 0% of each run, Pallas kernels for 0% -> 0%
where the time goes in v2:
time: 101 us
  blocking collectives  45.4 us (45%)
  Pallas kernels  25.6 us (25%)
  starting transfers between devices  24.4 us (24%)
  waiting for transfers between devices  3.07 us (3%)
  local copies, waits for them, and re-layouts  2.01 us (2%)
    all_to_all x1, blocking collectives, local(): lax.all_to_all(jnp.broadcast_to(total[None], parts.shape), 'grid', 0, 0,...  23 us
    all_to_all x1, blocking collectives, local(): lax.all_to_all(both.reshape(chips, chunk, BLOCK), 'grid', 0, 0, axis_inde...  22.4 us
    ppermute x1, starting transfers between devices, local(): both = keep + lax.ppermute(send, 'grid', pairs)  20.5 us
    pallas_call x1, Pallas kernels, local(): pl.pallas_call(finish_kernel, out_shape=jax.ShapeDtypeStruct((rows, bands...  20.3 us
    pallas_call x1, Pallas kernels, local(): pl.pallas_call(lambda *refs: gram_kernel(scale, *refs), out_shape=jax.Sha...  5.28 us
    ppermute x1, starting transfers between devices, local(): other = lax.ppermute(mine, 'grid', pairs)  3.89 us
  transfers between devices with their start and end apart: 2, of which 2 were waited for; matrix products, arithmetic and copies ran while one was open for 0% of the time, Pallas kernels for 0%

profile of v2, /device:TPU:513, one launch (start us, length us, event | category | flops | bytes accessed | tf_op | source)
XLA Modules:
  0.0 100.9 jit_solution(6628766703064892888)
XLA Ops:
  0.0 5.3 %gram.1 = f32[16,128,128]{2,1,0:T(8,128)} custom-call(s32[5]{0:T(128)} %order_ref.1, f32[512,640]{1,0:T(8,128)} %psi_ref.1), custom_call_target="tpu_custom_call" | custom-call | tf_op jit(solution)/shard_map/gram/pallas_call | solution.py:271
  5.3 0.0 copy-start
  5.3 1.2 %dynamic-slice_bitcast_fusion = f32[8,128,128]{2,1,0:T(8,128)S(1)} fusion(f32[2,8,128,128]{3,2,1,0:T(8,128)} %bitcast.8, s32[]{:T(128)S(6)} %select_n.16), kind=kLoop, calls=%fused_computation.1 | loop fusion | bytes 1048580 | tf_op jit(solution)/shard_map/jit(dynamic_index_in_dim)/squeeze | solution.py:285
  6.5 20.5 %collective-permute-start = (f32[8,128,128]{2,1,0:T(8,128)S(1)}, f32[8,128,128]{2,1,0:T(8,128)S(1)}, u32[]{:S(2)}, u32[]{:S(2)}) collective-permute-start(f32[8,128,128]{2,1,0:T(8,128)S(1)} %dynamic-slice_bitcast_fusion), channel_id=1, source_target_pairs={{0,1},{1,0},{2,3},{3,2},{4,5},{5,4},{6,7},{7,6},{8,9},{9,8},{10,11... | collective-permute-start | bytes 1572872 | tf_op jit(solution)/shard_map/ppermute | solution.py:286
  27.0 1.5 %collective-permute-done = f32[8,128,128]{2,1,0:T(8,128)S(1)} collective-permute-done((f32[8,128,128]{2,1,0:T(8,128)S(1)}, f32[8,128,128]{2,1,0:T(8,128)S(1)}, u32[]{:S(2)}, u32[]{:S(2)}) %collective-permute-start) | collective-permute-done | bytes 524320 | tf_op jit(solution)/shard_map/ppermute | solution.py:286
  28.5 0.0 copy-done
  28.5 0.1 bitcast_add_fusion
  28.6 22.4 %all_to_all.10 = f32[64,16,128]{2,1,0:T(8,128)S(1)} all-to-all(f32[64,16,128]{2,1,0:T(8,128)S(1)} %bitcast.10), channel_id=1, replica_groups={{0,2,4,6,8,10,12,14,16,18,20,22,24,26,28,30,32,34,36,38,40,42,44,46,48,..., dimensions={0} | all-to-all | bytes 1048576 | tf_op jit(solution)/shard_map/all_to_all | solution.py:287
  51.0 0.1 reduce_sum.9
  51.1 23.0 %all_to_all.11 = f32[64,16,128]{2,1,0:T(8,128)S(1)} all-to-all(f32[64,16,128]{2,1,0:T(8,128)S(1)} %broadcast_in_dim.2), channel_id=1, replica_groups={{0,2,4,6,8,10,12,14,16,18,20,22,24,26,28,30,32,34,36,38,40,42,44,46,48,..., dimensions={0} | all-to-all | bytes 1048576 | tf_op jit(solution)/shard_map/all_to_all | solution.py:291
  74.2 0.0 copy-start.1
  74.2 3.9 %collective-permute-start.1 = (f32[8,128,128]{2,1,0:T(8,128)S(1)}, f32[8,128,128]{2,1,0:T(8,128)S(1)}, u32[]{:S(2)}, u32[]{:S(2)}) collective-permute-start(f32[8,128,128]{2,1,0:T(8,128)S(1)} %bitcast.11), channel_id=1, source_target_pairs={{0,1},{1,0},{2,3},{3,2},{4,5},{5,4},{6,7},{7,6},{8,9},{9,8},{10,11... | collective-permute-start | bytes 1572872 | tf_op jit(solution)/shard_map/ppermute | solution.py:294
  78.0 1.5 %collective-permute-done.1.other_ref = f32[8,128,128]{2,1,0:T(8,128)S(1)} collective-permute-done((f32[8,128,128]{2,1,0:T(8,128)S(1)}, f32[8,128,128]{2,1,0:T(8,128)S(1)}, u32[]{:S(2)}, u32[]{:S(2)}) %collective-permute-start.1) | collective-permute-done | bytes 524320 | tf_op jit(solution)/shard_map/ppermute | solution.py:294
  79.6 0.0 copy-start.2
  79.6 0.0 copy-done.1
  79.6 0.8 copy-done.2
  80.4 20.3 %finish.1 = f32[512,640]{1,0:T(8,128)} custom-call(s32[1]{0:T(128)} %bitcast.core_ref, s32[5]{0:T(128)} %order_ref.1, f32[8,128,128]{2,1,0:T(8,128)} %bitcast.12, f32[8,128,128]{2,1,0:T(8,128)} %copy-done.2, f32[512,640]{1,0:T(8,128)} %psi_ref.1), custom_call_target="tpu_custom_call" | custom-call | tf_op jit(solution)/shard_map/finish/pallas_call | solution.py:296
  (1 shorter events, 0.0 us)
Async XLA Ops:
  5.3 23.3 %copy-start = (f32[16,128,128]{2,1,0:T(8,128)S(1)}, f32[16,128,128]{2,1,0:T(8,128)}, u32[]{:S(2)}) copy-start(f32[16,128,128]{2,1,0:T(8,128)} %gram.1) | copy-start | bytes 3145732
  6.5 22.1 %collective-permute-start = (f32[8,128,128]{2,1,0:T(8,128)S(1)}, f32[8,128,128]{2,1,0:T(8,128)S(1)}, u32[]{:S(2)}, u32[]{:S(2)}) collective-permute-start(f32[8,128,128]{2,1,0:T(8,128)S(1)} %dynamic-slice_bitcast_fusion), channel_id=1, source_target_pairs={{0,1},{1,0},{2,3},{3,2},{4,5},{5,4},{6,7},{7,6},{8,9},{9,8},{10,11... | collective-permute-start | bytes 1572872 | tf_op jit(solution)/shard_map/ppermute | solution.py:286
  74.2 5.4 %copy-start.1 = (f32[64,16,128]{2,1,0:T(8,128)}, f32[64,16,128]{2,1,0:T(8,128)S(1)}, u32[]{:S(2)}) copy-start(f32[64,16,128]{2,1,0:T(8,128)S(1)} %all_to_all.11) | copy-start | bytes 1572868
  74.2 5.4 %collective-permute-start.1 = (f32[8,128,128]{2,1,0:T(8,128)S(1)}, f32[8,128,128]{2,1,0:T(8,128)S(1)}, u32[]{:S(2)}, u32[]{:S(2)}) collective-permute-start(f32[8,128,128]{2,1,0:T(8,128)S(1)} %bitcast.11), channel_id=1, source_target_pairs={{0,1},{1,0},{2,3},{3,2},{4,5},{5,4},{6,7},{7,6},{8,9},{9,8},{10,11... | collective-permute-start | bytes 1572872 | tf_op jit(solution)/shard_map/ppermute | solution.py:294
  79.6 0.8 copy-start.2

commit v3 on v2

--- a/solution.py
+++ b/solution.py
@@ -51,12 +51,10 @@
     return copies
 
 
-def gram_kernel(scale, order_ref, psi_ref, out_ref, x_ref, sems):
-    loads = block_copies(order_ref, psi_ref, x_ref, sems)
-    for load in loads:
-        load.start()
-    for load in loads:
-        load.wait()
+def gram_kernel(scale, order_ref, psi_ref, out_ref, x_ref):
+    for i in range(NBLK):
+        start = pl.multiple_of(order_ref[i] * BLOCK, BLOCK)
+        x_ref[:, span(i, i + 1)] = psi_ref[:, pl.ds(start, BLOCK)]
     for i in range(NBLK):
         row = dot_tn(x_ref[:, span(i, i + 1)], x_ref[:, i * BLOCK:]) * scale
         for j in range(i, NBLK):
@@ -270,13 +268,10 @@
 
     gram = pl.pallas_call(
         lambda *refs: gram_kernel(scale, *refs),
-        out_shape=jax.ShapeDtypeStruct((SLOTS, BLOCK, BLOCK), jnp.float32),
-        in_specs=[smem(), anywhere()],
+        out_shape=pltpu.VMEM((SLOTS, BLOCK, BLOCK), jnp.float32),
+        in_specs=[smem(), vmem()],
         out_specs=vmem(),
-        scratch_shapes=[
-            pltpu.VMEM((rows, bands), jnp.float32),
-            pltpu.SemaphoreType.DMA((NBLK,)),
-        ],
+        scratch_shapes=[pltpu.VMEM((rows, bands), jnp.float32)],
         name="gram",
     )(order, psi)
 
@@ -292,6 +287,8 @@
         jnp.broadcast_to(total[None], parts.shape), "grid", 0, 0, axis_index_groups=groups, tiled=True
     ).reshape(half, BLOCK, BLOCK)
     other = lax.ppermute(mine, "grid", pairs)
+    mine = pltpu.with_memory_space_constraint(mine, pltpu.VMEM)
+    other = pltpu.with_memory_space_constraint(other, pltpu.VMEM)
 
     return pl.pallas_call(
         finish_kernel,

time: 101 us -> 97 us (0.960)
  Pallas kernels: 25.6 us -> 23.5 us
  local copies, waits for them, and re-layouts: 2.01 us -> 0.08 us
    pallas_call x1, Pallas kernels: 5.28 us -> 3.53 us  [local(): pl.pallas_call(lambda *refs: gram_kernel(scale, *refs), out_shape=pltpu.V...]
    squeeze x1, local copies, waits for them, and re-layouts: 1.17 us -> 0.04 us  [local(): send = lax.dynamic_index_in_dim(gram, 1 - core, 0, keepdims=False)]
where the time goes in v3:
time: 97 us; the launch traced here: 96.8 us
  blocking collectives  45.4 us (47%)
  starting transfers between devices  24.4 us (25%)
  Pallas kernels  23.5 us (24%)
  waiting for transfers between devices  3.07 us (3%)
    all_to_all x1, blocking collectives, local(): lax.all_to_all(jnp.broadcast_to(total[None], parts.shape), 'grid', 0, 0,...  23 us
    all_to_all x1, blocking collectives, local(): lax.all_to_all(both.reshape(chips, chunk, BLOCK), 'grid', 0, 0, axis_inde...  22.4 us
    ppermute x1, starting transfers between devices, local(): both = keep + lax.ppermute(send, 'grid', pairs)  20.5 us
    pallas_call x1, Pallas kernels, local(): pl.pallas_call(finish_kernel, out_shape=jax.ShapeDtypeStruct((rows, bands...  19.9 us
    ppermute x1, starting transfers between devices, local(): other = lax.ppermute(mine, 'grid', pairs)  3.89 us
    pallas_call x1, Pallas kernels, local(): pl.pallas_call(lambda *refs: gram_kernel(scale, *refs), out_shape=pltpu.V...  3.53 us
  transfers between devices with their start and end apart: 2, of which 2 were waited for; matrix products, arithmetic and copies ran while one was open for 0% of the time, Pallas kernels for 0%

profile of v3, /device:TPU:513, one launch (start us, length us, event | category | flops | bytes accessed | tf_op | source)
XLA Modules:
  0.0 96.8 jit_solution(17818394917007986389)
XLA Ops:
  0.0 3.5 %gram.1 = f32[16,128,128]{2,1,0:T(8,128)S(1)} custom-call(s32[5]{0:T(128)} %order_ref.1, f32[512,640]{1,0:T(8,128)} %psi_ref.1), custom_call_target="tpu_custom_call" | custom-call | tf_op jit(solution)/shard_map/gram/pallas_call | solution.py:269
  3.6 20.5 %collective-permute-start = (f32[8,128,128]{2,1,0:T(8,128)S(1)}, f32[8,128,128]{2,1,0:T(8,128)S(1)}, u32[]{:S(2)}, u32[]{:S(2)}) collective-permute-start(f32[8,128,128]{2,1,0:T(8,128)S(1)} %dynamic-slice_bitcast_fusion), channel_id=1, source_target_pairs={{0,1},{1,0},{2,3},{3,2},{4,5},{5,4},{6,7},{7,6},{8,9},{9,8},{10,11... | collective-permute-start | bytes 1572872 | tf_op jit(solution)/shard_map/ppermute | solution.py:281
  24.1 1.5 %collective-permute-done = f32[8,128,128]{2,1,0:T(8,128)S(1)} collective-permute-done((f32[8,128,128]{2,1,0:T(8,128)S(1)}, f32[8,128,128]{2,1,0:T(8,128)S(1)}, u32[]{:S(2)}, u32[]{:S(2)}) %collective-permute-start) | collective-permute-done | bytes 524320 | tf_op jit(solution)/shard_map/ppermute | solution.py:281
  25.7 0.1 bitcast_add_fusion
  25.7 22.4 %all_to_all.10 = f32[64,16,128]{2,1,0:T(8,128)S(1)} all-to-all(f32[64,16,128]{2,1,0:T(8,128)S(1)} %bitcast.12), channel_id=1, replica_groups={{0,2,4,6,8,10,12,14,16,18,20,22,24,26,28,30,32,34,36,38,40,42,44,46,48,..., dimensions={0} | all-to-all | bytes 1048576 | tf_op jit(solution)/shard_map/all_to_all | solution.py:282
  48.1 0.1 reduce_sum.9
  48.3 23.0 %all_to_all.11 = f32[64,16,128]{2,1,0:T(8,128)S(1)} all-to-all(f32[64,16,128]{2,1,0:T(8,128)S(1)} %broadcast_in_dim.2), channel_id=1, replica_groups={{0,2,4,6,8,10,12,14,16,18,20,22,24,26,28,30,32,34,36,38,40,42,44,46,48,..., dimensions={0} | all-to-all | bytes 1048576 | tf_op jit(solution)/shard_map/all_to_all | solution.py:286
  71.3 3.9 %collective-permute-start.1 = (f32[8,128,128]{2,1,0:T(8,128)S(1)}, f32[8,128,128]{2,1,0:T(8,128)S(1)}, u32[]{:S(2)}, u32[]{:S(2)}) collective-permute-start(f32[8,128,128]{2,1,0:T(8,128)S(1)} %bitcast.10), channel_id=1, source_target_pairs={{0,1},{1,0},{2,3},{3,2},{4,5},{5,4},{6,7},{7,6},{8,9},{9,8},{10,11... | collective-permute-start | bytes 1572872 | tf_op jit(solution)/shard_map/ppermute | solution.py:289
  75.2 1.5 %collective-permute-done.1.other_ref = f32[8,128,128]{2,1,0:T(8,128)S(1)} collective-permute-done((f32[8,128,128]{2,1,0:T(8,128)S(1)}, f32[8,128,128]{2,1,0:T(8,128)S(1)}, u32[]{:S(2)}, u32[]{:S(2)}) %collective-permute-start.1) | collective-permute-done | bytes 524320 | tf_op jit(solution)/shard_map/ppermute | solution.py:289
  76.7 19.9 %finish.1 = f32[512,640]{1,0:T(8,128)} custom-call(s32[1]{0:T(128)} %bitcast.core_ref, s32[5]{0:T(128)} %order_ref.1, f32[8,128,128]{2,1,0:T(8,128)S(1)} %bitcast.11, f32[8,128,128]{2,1,0:T(8,128)S(1)} %collective-permute-done.1.other_ref, f32[512,640]{1,0:T(8,128)} %psi_ref.1), custom_call_target="tpu_custom_call" | custom-call | tf_op jit(solution)/shard_map/finish/pallas_call | solution.py:293
  (2 shorter events, 0.1 us)
Async XLA Ops:
  3.6 22.1 %collective-permute-start = (f32[8,128,128]{2,1,0:T(8,128)S(1)}, f32[8,128,128]{2,1,0:T(8,128)S(1)}, u32[]{:S(2)}, u32[]{:S(2)}) collective-permute-start(f32[8,128,128]{2,1,0:T(8,128)S(1)} %dynamic-slice_bitcast_fusion), channel_id=1, source_target_pairs={{0,1},{1,0},{2,3},{3,2},{4,5},{5,4},{6,7},{7,6},{8,9},{9,8},{10,11... | collective-permute-start | bytes 1572872 | tf_op jit(solution)/shard_map/ppermute | solution.py:281
  71.3 5.4 %collective-permute-start.1 = (f32[8,128,128]{2,1,0:T(8,128)S(1)}, f32[8,128,128]{2,1,0:T(8,128)S(1)}, u32[]{:S(2)}, u32[]{:S(2)}) collective-permute-start(f32[8,128,128]{2,1,0:T(8,128)S(1)} %bitcast.10), channel_id=1, source_target_pairs={{0,1},{1,0},{2,3},{3,2},{4,5},{5,4},{6,7},{7,6},{8,9},{9,8},{10,11... | collective-permute-start | bytes 1572872 | tf_op jit(solution)/shard_map/ppermute | solution.py:289

commit v4 on v3

--- a/solution.py
+++ b/solution.py
@@ -9,6 +9,7 @@
 NBLK = 5
 PANEL = 32
 SUB = 8
+PANELS = BLOCK // PANEL
 PAIRS = [(i, j) for i in range(NBLK) for j in range(i, NBLK)]
 SLOT = {pair: slot for slot, pair in enumerate(PAIRS)}
 SLOTS = 16
@@ -63,11 +64,11 @@
         out_ref[extra] = jnp.zeros((BLOCK, BLOCK), jnp.float32)
 
 
-def eliminate(work_ref, col_ref, between):
+def eliminate(work_ref, col_ref, after_panel):
     lane = lax.broadcasted_iota(jnp.int32, (SUB, BLOCK), 1)
     row = lax.broadcasted_iota(jnp.int32, (SUB, BLOCK), 0)
     pieces = PANEL // SUB
-    for p in range(BLOCK // PANEL):
+    for p in range(PANELS):
         r0 = p * PANEL
         low = r0 + PANEL
         for m in range(PANEL):
@@ -101,22 +102,27 @@
             part[kq] = part[kq] - jnp.where(row > ks, factor[kq], 0.0) * lead
             for q in range(kq + 1, pieces):
                 part[q] = part[q] - factor[q] * lead
-        whole = jnp.concatenate([part[q] * lax.rsqrt(diag[q]) for q in range(pieces)], axis=0)
-        work_ref[r0:low, :] = whole
+        work_ref[r0:low, :] = jnp.concatenate(
+            [part[q] * lax.rsqrt(diag[q]) for q in range(pieces)], axis=0
+        )
         if low < BLOCK:
-            update = dot(whole.T[low:, :], whole)
-            rest = lax.broadcasted_iota(jnp.int32, (BLOCK - low, BLOCK), 1)
-            kept = jnp.where((rest >= r0) & (rest < low), 0.0, work_ref[low:, :])
-            work_ref[low:, :] = kept - update
-        between()
+            turned = jnp.concatenate(part, axis=0).T
+            scaled = jnp.concatenate([part[q] * (1.0 / diag[q]) for q in range(pieces)], axis=0)
+            for first, last in ((low, low + PANEL), (low + PANEL, BLOCK)):
+                if first < last:
+                    rest = lax.broadcasted_iota(jnp.int32, (last - first, BLOCK), 1)
+                    kept = jnp.where((rest >= r0) & (rest < low), 0.0, work_ref[first:last, :])
+                    work_ref[first:last, :] = kept - dot(turned[first:last, :], scaled)
+        after_panel(p)
 
 
 def finish_kernel(
     core_ref, order_ref, mine_ref, other_ref, psi_ref, out_ref,
-    a_ref, inv_ref, pair_ref, x_ref, q_ref, work_ref, col_ref, in_sems, out_sems,
+    a_ref, inv_ref, pair_ref, x_ref, q_ref, work_ref, next_ref, col_ref, in_sems, out_sems,
 ):
     loads = block_copies(order_ref, psi_ref, x_ref, in_sems)
     stores = block_copies(order_ref, out_ref, q_ref, out_sems, outward=True)
+    final = NBLK - 1
     for load in loads:
         load.start()
     core = core_ref[0]
@@ -133,6 +139,15 @@
     rows = x_ref.shape[0]
     tiles = [slice(r, r + BLOCK) for r in range(0, rows, BLOCK)]
     soon, whenever = [], []
+    where_to = pl.multiple_of(order_ref[final] * BLOCK, BLOCK)
+    stores = stores[:final] + [
+        pltpu.make_async_copy(
+            q_ref.at[tile, span(final, NBLK)],
+            out_ref.at[tile, pl.ds(where_to, BLOCK)],
+            out_sems.at[final + t],
+        )
+        for t, tile in enumerate(tiles)
+    ]
 
     def a(i, j, wide=1):
         return a_ref[span(i, i + 1), span(j, j + wide)]
@@ -168,12 +183,18 @@
         for b in range(first, last):
             stores[b].start()
 
+    def solve_rows(k, p, work):
+        rows = slice(k * BLOCK + p * PANEL, k * BLOCK + (p + 1) * PANEL)
+        lane = lax.broadcasted_iota(jnp.int32, (PANEL, BLOCK), 1)
+        left = jnp.where(lane < (p + 1) * PANEL, work[p * PANEL:(p + 1) * PANEL, :], 0.0)
+        value = dot(left, original[...])
+        a_ref[rows, span(k + 1, k + 2)] = value
+        return value
+
     def after(k):
+        first = k // 2 * 2
         if k + 1 == NBLK:
             return
-        solve(k, k + 1)
-        downdate(k + 1, k + 1, k, k + 1)
-        first = k // 2 * 2
         if k % 2 == 0:
             soon.append(lambda: couple(k))
             if k + 2 < NBLK:
@@ -200,30 +221,45 @@
         for _ in range(min(count, len(queue))):
             queue.pop(0)()
 
-    panels = BLOCK // PANEL
+    work_ref[0] = a(0, 0)
     for k in range(NBLK):
-        work_ref[...] = a(k, k)
-        state = {"left": panels}
-
-        def between():
-            run(soon, -(-len(soon) // max(state["left"] - 1, 1)))
-            more = panels if k % 2 == 0 and k + 1 < NBLK else 0
-            turns = state["left"] + more
+        work = work_ref.at[k % 2]
+        following = work_ref.at[1 - k % 2]
+        original = next_ref.at[k % 2]
+        more = k + 1 < NBLK
+        early = (PANELS - 1) * PANEL
+
+        def after_panel(p):
+            if p == PANELS - 1:
+                return
+            left = PANELS - 1 - p
+            run(soon, -(-len(soon) // max(left - 1, 1)))
+            if p == PANELS - 2:
+                run(soon, len(soon))
+                if more:
+                    original[...] = a(k, k + 1)
+                    for done in range(PANELS - 1):
+                        solve_rows(k, done, work)
+                    solved = a_ref[k * BLOCK:k * BLOCK + early, span(k + 1, k + 2)]
+                    following[...] = a(k + 1, k + 1) - dot_tn(solved, solved)
+            turns = left + (PANELS - 1 if k % 2 == 0 and more else 0)
             run(whenever, -(-len(whenever) // turns))
-            state["left"] -= 1
-
-        eliminate(work_ref, col_ref, between)
-        run(soon, len(soon))
-        inv_ref[k] = jnp.where(lower, work_ref[...], 0.0)
+
+        eliminate(work, col_ref, after_panel)
+        if more:
+            value = solve_rows(k, PANELS - 1, work)
+            turned = value.T
+            for first, last in ((0, PANEL), (PANEL, BLOCK)):
+                following[first:last, :] = following[first:last, :] - dot(turned[first:last, :], value)
+        inv_ref[k] = jnp.where(lower, work[...], 0.0)
         if k == 1:
             for load in loads:
                 load.wait()
         after(k)
     run(whenever, len(whenever))
-    last = NBLK - 1
-    for tile in tiles:
-        finish(last, 1, tile)
-    send(last, NBLK)
+    for t, tile in enumerate(tiles):
+        finish(final, 1, tile)
+        stores[final + t].start()
     for store in stores:
         store.wait()
 
@@ -248,10 +284,11 @@
         pltpu.VMEM((NBLK, 2 * BLOCK, 2 * BLOCK), jnp.float32),
         pltpu.VMEM((rows, bands), jnp.float32),
         pltpu.VMEM((rows, bands), jnp.float32),
-        pltpu.VMEM((BLOCK, BLOCK), jnp.float32),
+        pltpu.VMEM((2, BLOCK, BLOCK), jnp.float32),
+        pltpu.VMEM((2, BLOCK, BLOCK), jnp.float32),
         pltpu.VMEM((PANEL, PANEL, BLOCK), jnp.float32),
         pltpu.SemaphoreType.DMA((NBLK,)),
-        pltpu.SemaphoreType.DMA((NBLK,)),
+        pltpu.SemaphoreType.DMA((NBLK - 1 + rows // BLOCK,)),
     ]
 
 

time: 97 us -> 97.5 us (level)
  no operation moved by 1% of the time
where the time goes in v4:
time: 97.5 us; the launch traced here: 97.3 us
  blocking collectives  45.4 us (47%)
  starting transfers between devices  24.4 us (25%)
  Pallas kernels  23.9 us (25%)
  waiting for transfers between devices  3.07 us (3%)
    all_to_all x1, blocking collectives, local(): lax.all_to_all(jnp.broadcast_to(total[None], parts.shape), 'grid', 0, 0,...  23 us
    all_to_all x1, blocking collectives, local(): lax.all_to_all(both.reshape(chips, chunk, BLOCK), 'grid', 0, 0, axis_inde...  22.4 us
    ppermute x1, starting transfers between devices, local(): both = keep + lax.ppermute(send, 'grid', pairs)  20.5 us
    pallas_call x1, Pallas kernels, local(): pl.pallas_call(finish_kernel, out_shape=jax.ShapeDtypeStruct((rows, bands...  20.4 us
    ppermute x1, starting transfers between devices, local(): other = lax.ppermute(mine, 'grid', pairs)  3.89 us
    pallas_call x1, Pallas kernels, local(): pl.pallas_call(lambda *refs: gram_kernel(scale, *refs), out_shape=pltpu.V...  3.53 us
  transfers between devices with their start and end apart: 2, of which 2 were waited for; matrix products, arithmetic and copies ran while one was open for 0% of the time, Pallas kernels for 0%

profile of v4, /device:TPU:513, one launch (start us, length us, event | category | flops | bytes accessed | tf_op | source)
XLA Modules:
  0.0 97.3 jit_solution(17257787701636522605)
XLA Ops:
  0.0 3.5 %gram.1 = f32[16,128,128]{2,1,0:T(8,128)S(1)} custom-call(s32[5]{0:T(128)} %order_ref.1, f32[512,640]{1,0:T(8,128)} %psi_ref.1), custom_call_target="tpu_custom_call" | custom-call | tf_op jit(solution)/shard_map/gram/pallas_call | solution.py:306
  3.6 20.5 %collective-permute-start = (f32[8,128,128]{2,1,0:T(8,128)S(1)}, f32[8,128,128]{2,1,0:T(8,128)S(1)}, u32[]{:S(2)}, u32[]{:S(2)}) collective-permute-start(f32[8,128,128]{2,1,0:T(8,128)S(1)} %dynamic-slice_bitcast_fusion), channel_id=1, source_target_pairs={{0,1},{1,0},{2,3},{3,2},{4,5},{5,4},{6,7},{7,6},{8,9},{9,8},{10,11... | collective-permute-start | bytes 1572872 | tf_op jit(solution)/shard_map/ppermute | solution.py:318
  24.1 1.5 %collective-permute-done = f32[8,128,128]{2,1,0:T(8,128)S(1)} collective-permute-done((f32[8,128,128]{2,1,0:T(8,128)S(1)}, f32[8,128,128]{2,1,0:T(8,128)S(1)}, u32[]{:S(2)}, u32[]{:S(2)}) %collective-permute-start) | collective-permute-done | bytes 524320 | tf_op jit(solution)/shard_map/ppermute | solution.py:318
  25.7 0.1 bitcast_add_fusion
  25.7 22.4 %all_to_all.10 = f32[64,16,128]{2,1,0:T(8,128)S(1)} all-to-all(f32[64,16,128]{2,1,0:T(8,128)S(1)} %bitcast.12), channel_id=1, replica_groups={{0,2,4,6,8,10,12,14,16,18,20,22,24,26,28,30,32,34,36,38,40,42,44,46,48,..., dimensions={0} | all-to-all | bytes 1048576 | tf_op jit(solution)/shard_map/all_to_all | solution.py:319
  48.1 0.1 reduce_sum.9
  48.2 23.0 %all_to_all.11 = f32[64,16,128]{2,1,0:T(8,128)S(1)} all-to-all(f32[64,16,128]{2,1,0:T(8,128)S(1)} %broadcast_in_dim.2), channel_id=1, replica_groups={{0,2,4,6,8,10,12,14,16,18,20,22,24,26,28,30,32,34,36,38,40,42,44,46,48,..., dimensions={0} | all-to-all | bytes 1048576 | tf_op jit(solution)/shard_map/all_to_all | solution.py:323
  71.3 3.9 %collective-permute-start.1 = (f32[8,128,128]{2,1,0:T(8,128)S(1)}, f32[8,128,128]{2,1,0:T(8,128)S(1)}, u32[]{:S(2)}, u32[]{:S(2)}) collective-permute-start(f32[8,128,128]{2,1,0:T(8,128)S(1)} %bitcast.10), channel_id=1, source_target_pairs={{0,1},{1,0},{2,3},{3,2},{4,5},{5,4},{6,7},{7,6},{8,9},{9,8},{10,11... | collective-permute-start | bytes 1572872 | tf_op jit(solution)/shard_map/ppermute | solution.py:326
  75.2 1.5 %collective-permute-done.1.other_ref = f32[8,128,128]{2,1,0:T(8,128)S(1)} collective-permute-done((f32[8,128,128]{2,1,0:T(8,128)S(1)}, f32[8,128,128]{2,1,0:T(8,128)S(1)}, u32[]{:S(2)}, u32[]{:S(2)}) %collective-permute-start.1) | collective-permute-done | bytes 524320 | tf_op jit(solution)/shard_map/ppermute | solution.py:326
  76.7 20.4 %finish.1 = f32[512,640]{1,0:T(8,128)} custom-call(s32[1]{0:T(128)} %bitcast.core_ref, s32[5]{0:T(128)} %order_ref.1, f32[8,128,128]{2,1,0:T(8,128)S(1)} %bitcast.11, f32[8,128,128]{2,1,0:T(8,128)S(1)} %collective-permute-done.1.other_ref, f32[512,640]{1,0:T(8,128)} %psi_ref.1), custom_call_target="tpu_custom_call" | custom-call | tf_op jit(solution)/shard_map/finish/pallas_call | solution.py:330
  (2 shorter events, 0.1 us)
Async XLA Ops:
  3.6 22.1 %collective-permute-start = (f32[8,128,128]{2,1,0:T(8,128)S(1)}, f32[8,128,128]{2,1,0:T(8,128)S(1)}, u32[]{:S(2)}, u32[]{:S(2)}) collective-permute-start(f32[8,128,128]{2,1,0:T(8,128)S(1)} %dynamic-slice_bitcast_fusion), channel_id=1, source_target_pairs={{0,1},{1,0},{2,3},{3,2},{4,5},{5,4},{6,7},{7,6},{8,9},{9,8},{10,11... | collective-permute-start | bytes 1572872 | tf_op jit(solution)/shard_map/ppermute | solution.py:318
  71.3 5.4 %collective-permute-start.1 = (f32[8,128,128]{2,1,0:T(8,128)S(1)}, f32[8,128,128]{2,1,0:T(8,128)S(1)}, u32[]{:S(2)}, u32[]{:S(2)}) collective-permute-start(f32[8,128,128]{2,1,0:T(8,128)S(1)} %bitcast.10), channel_id=1, source_target_pairs={{0,1},{1,0},{2,3},{3,2},{4,5},{5,4},{6,7},{7,6},{8,9},{9,8},{10,11... | collective-permute-start | bytes 1572872 | tf_op jit(solution)/shard_map/ppermute | solution.py:326

commit v5 on v4

--- a/solution.py
+++ b/solution.py
@@ -38,9 +38,9 @@
     return slice(first * BLOCK, last * BLOCK)
 
 
-def block_copies(order_ref, far_ref, near_ref, sems, outward=False):
+def block_copies(order_ref, far_ref, near_ref, sems, count, outward=False):
     copies = []
-    for b in range(NBLK):
+    for b in range(count):
         start = pl.multiple_of(order_ref[b] * BLOCK, BLOCK)
         far = far_ref.at[:, pl.ds(start, BLOCK)]
         near = near_ref.at[:, span(b, b + 1)]
@@ -60,11 +60,10 @@
         row = dot_tn(x_ref[:, span(i, i + 1)], x_ref[:, i * BLOCK:]) * scale
         for j in range(i, NBLK):
             out_ref[SLOT[i, j]] = row[:, span(j - i, j - i + 1)]
-    for extra in range(len(PAIRS), SLOTS):
-        out_ref[extra] = jnp.zeros((BLOCK, BLOCK), jnp.float32)
-
-
-def eliminate(work_ref, col_ref, after_panel):
+    out_ref[SLOTS - 1] = out_ref[0]
+
+
+def eliminate(work_ref, col_ref, row_ref, after_panel):
     lane = lax.broadcasted_iota(jnp.int32, (SUB, BLOCK), 1)
     row = lax.broadcasted_iota(jnp.int32, (SUB, BLOCK), 0)
     pieces = PANEL // SUB
@@ -81,27 +80,33 @@
         for q in range(pieces):
             unit = (lane == row + (r0 + q * SUB)).astype(jnp.float32)
             part.append(jnp.where(inside, unit, work_ref[r0 + q * SUB:r0 + (q + 1) * SUB, :]))
-        column = {
-            (m, q): col_ref[m, q * SUB:(q + 1) * SUB, :]
-            for m in range(PANEL)
-            for q in range(m // SUB, pieces)
-        }
         diag = [jnp.ones((SUB, BLOCK), jnp.float32)] * pieces
-        for k in range(PANEL):
-            kq, ks = divmod(k, SUB)
-            pivot = column[k, kq][ks:ks + 1, :]
-            inverse = 1.0 / pivot
-            diag[kq] = jnp.where(row == ks, pivot, diag[kq])
-            factor = {q: column[k, q] * inverse for q in range(kq, pieces)}
-            for m in range(k + 1, PANEL):
-                mq, ms = divmod(m, SUB)
-                entry = column[k, mq][ms:ms + 1, :]
-                for q in range(mq, pieces):
-                    column[m, q] = column[m, q] - factor[q] * entry
-            lead = part[kq][ks:ks + 1, :]
-            part[kq] = part[kq] - jnp.where(row > ks, factor[kq], 0.0) * lead
-            for q in range(kq + 1, pieces):
-                part[q] = part[q] - factor[q] * lead
+        factors = {}
+        for group in range(pieces):
+            column = {}
+            for m in range(group * SUB, (group + 1) * SUB):
+                for q in range(group, pieces):
+                    value = col_ref[m, q * SUB:(q + 1) * SUB, :]
+                    for k in range(group * SUB):
+                        value = value - factors[k, q] * row_ref[k, m:m + 1, :]
+                    column[m, q] = value
+            for k in range(group * SUB, (group + 1) * SUB):
+                ks = k % SUB
+                pivot = column[k, group][ks:ks + 1, :]
+                inverse = 1.0 / pivot
+                diag[group] = jnp.where(row == ks, pivot, diag[group])
+                for q in range(group, pieces):
+                    factors[k, q] = column[k, q] * inverse
+                for q in range(group + 1, pieces):
+                    row_ref[k, q * SUB:(q + 1) * SUB, :] = column[k, q]
+                for m in range(k + 1, (group + 1) * SUB):
+                    entry = column[k, group][m % SUB:m % SUB + 1, :]
+                    for q in range(group, pieces):
+                        column[m, q] = column[m, q] - factors[k, q] * entry
+                lead = part[group][ks:ks + 1, :]
+                part[group] = part[group] - jnp.where(row > ks, factors[k, group], 0.0) * lead
+                for q in range(group + 1, pieces):
+                    part[q] = part[q] - factors[k, q] * lead
         work_ref[r0:low, :] = jnp.concatenate(
             [part[q] * lax.rsqrt(diag[q]) for q in range(pieces)], axis=0
         )
@@ -116,13 +121,19 @@
         after_panel(p)
 
 
+def lead_kernel(core_ref, mine_ref, out_ref, work_ref, col_ref, row_ref):
+    work_ref[...] = jnp.where(core_ref[0] == 0, mine_ref[0], mine_ref[SLOTS // 2 - 1])
+    eliminate(work_ref, col_ref, row_ref, lambda p: None)
+    out_ref[...] = work_ref[...]
+
+
 def finish_kernel(
-    core_ref, order_ref, mine_ref, other_ref, psi_ref, out_ref,
-    a_ref, inv_ref, pair_ref, x_ref, q_ref, work_ref, next_ref, col_ref, in_sems, out_sems,
+    core_ref, order_ref, lead_ref, mine_ref, other_ref, psi_ref, out_ref,
+    a_ref, inv_ref, pair_ref, x_ref, q_ref, work_ref, next_ref, col_ref, row_ref, in_sems, out_sems,
 ):
-    loads = block_copies(order_ref, psi_ref, x_ref, in_sems)
-    stores = block_copies(order_ref, out_ref, q_ref, out_sems, outward=True)
+    loads = block_copies(order_ref, psi_ref, x_ref, in_sems, NBLK)
     final = NBLK - 1
+    stores = block_copies(order_ref, out_ref, q_ref, out_sems, final, outward=True)
     for load in loads:
         load.start()
     core = core_ref[0]
@@ -140,7 +151,7 @@
     tiles = [slice(r, r + BLOCK) for r in range(0, rows, BLOCK)]
     soon, whenever = [], []
     where_to = pl.multiple_of(order_ref[final] * BLOCK, BLOCK)
-    stores = stores[:final] + [
+    stores = stores + [
         pltpu.make_async_copy(
             q_ref.at[tile, span(final, NBLK)],
             out_ref.at[tile, pl.ds(where_to, BLOCK)],
@@ -221,8 +232,15 @@
         for _ in range(min(count, len(queue))):
             queue.pop(0)()
 
-    work_ref[0] = a(0, 0)
-    for k in range(NBLK):
+    inv_ref[0] = jnp.where(lower, lead_ref[...], 0.0)
+    solve(0, 1)
+    turned = a(0, 1).T
+    for first, last in ((0, PANEL), (PANEL, BLOCK)):
+        work_ref[1, first:last, :] = a_ref[BLOCK + first:BLOCK + last, span(1, 2)] - dot(
+            turned[first:last, :], a(0, 1)
+        )
+    after(0)
+    for k in range(1, NBLK):
         work = work_ref.at[k % 2]
         following = work_ref.at[1 - k % 2]
         original = next_ref.at[k % 2]
@@ -245,7 +263,7 @@
             turns = left + (PANELS - 1 if k % 2 == 0 and more else 0)
             run(whenever, -(-len(whenever) // turns))
 
-        eliminate(work, col_ref, after_panel)
+        eliminate(work, col_ref, row_ref, after_panel)
         if more:
             value = solve_rows(k, PANELS - 1, work)
             turned = value.T
@@ -287,6 +305,7 @@
         pltpu.VMEM((2, BLOCK, BLOCK), jnp.float32),
         pltpu.VMEM((2, BLOCK, BLOCK), jnp.float32),
         pltpu.VMEM((PANEL, PANEL, BLOCK), jnp.float32),
+        pltpu.VMEM((PANEL, PANEL, BLOCK), jnp.float32),
         pltpu.SemaphoreType.DMA((NBLK,)),
         pltpu.SemaphoreType.DMA((NBLK - 1 + rows // BLOCK,)),
     ]
@@ -327,14 +346,28 @@
     mine = pltpu.with_memory_space_constraint(mine, pltpu.VMEM)
     other = pltpu.with_memory_space_constraint(other, pltpu.VMEM)
 
+    core = core.astype(jnp.int32).reshape(1)
+    lead = pl.pallas_call(
+        lead_kernel,
+        out_shape=pltpu.VMEM((BLOCK, BLOCK), jnp.float32),
+        in_specs=[smem(), vmem()],
+        out_specs=vmem(),
+        scratch_shapes=[
+            pltpu.VMEM((BLOCK, BLOCK), jnp.float32),
+            pltpu.VMEM((PANEL, PANEL, BLOCK), jnp.float32),
+            pltpu.VMEM((PANEL, PANEL, BLOCK), jnp.float32),
+        ],
+        name="lead",
+    )(core, mine)
+    lead = pltpu.with_memory_space_constraint(lead, pltpu.VMEM)
     return pl.pallas_call(
         finish_kernel,
         out_shape=jax.ShapeDtypeStruct((rows, bands), jnp.float32),
-        in_specs=[smem(), smem(), vmem(), vmem(), anywhere()],
+        in_specs=[smem(), smem(), vmem(), vmem(), vmem(), anywhere()],
         out_specs=anywhere(),
         scratch_shapes=finish_scratch(rows),
         name="finish",
-    )(core.astype(jnp.int32).reshape(1), order, mine, other, psi)
+    )(core, order, lead, mine, other, psi)
 
 
 def solution(mesh):

time: 97.5 us -> 95.3 us (0.977)
  waiting for transfers between devices: 3.07 us -> 1.54 us
    pallas_call x1, Pallas kernels: 20.4 us -> 17.1 us  [local(): pl.pallas_call(finish_kernel, out_shape=jax.ShapeDtypeStruct((rows, bands...]
    pallas_call x0 -> x1, Pallas kernels: none -> 2.64 us  [local(): pl.pallas_call(lead_kernel, out_shape=pltpu.VMEM((BLOCK, BLOCK), jnp.floa...]
    ppermute x1, waiting for transfers between devices: 1.54 us -> 0.01 us  [local(): other = lax.ppermute(mine, 'grid', pairs)]
  transfers between devices with their start and end apart: 2 -> 2, of which waited for: 2 -> 1; matrix products, arithmetic and copies ran while one was open for 0% -> 0% of each run, Pallas kernels for 0% -> 3%
where the time goes in v5:
time: 95.3 us; the launch traced here: 95.1 us
  blocking collectives  45.4 us (48%)
  starting transfers between devices  24.4 us (26%)
  Pallas kernels  23.3 us (24%)
  waiting for transfers between devices  1.54 us (2%)
    all_to_all x1, blocking collectives, local(): lax.all_to_all(jnp.broadcast_to(total[None], parts.shape), 'grid', 0, 0,...  23 us
    all_to_all x1, blocking collectives, local(): lax.all_to_all(both.reshape(chips, chunk, BLOCK), 'grid', 0, 0, axis_inde...  22.4 us
    ppermute x1, starting transfers between devices, local(): both = keep + lax.ppermute(send, 'grid', pairs)  20.5 us
    pallas_call x1, Pallas kernels, local(): pl.pallas_call(finish_kernel, out_shape=jax.ShapeDtypeStruct((rows, bands...  17.1 us
    ppermute x1, starting transfers between devices, local(): other = lax.ppermute(mine, 'grid', pairs)  3.89 us
    pallas_call x1, Pallas kernels, local(): pl.pallas_call(lambda *refs: gram_kernel(scale, *refs), out_shape=pltpu.V...  3.53 us
    pallas_call x1, Pallas kernels, local(): pl.pallas_call(lead_kernel, out_shape=pltpu.VMEM((BLOCK, BLOCK), jnp.floa...  2.64 us
  transfers between devices with their start and end apart: 2, of which 1 were waited for; matrix products, arithmetic and copies ran while one was open for 0% of the time, Pallas kernels for 3%

profile of v5, /device:TPU:513, one launch (start us, length us, event | category | flops | bytes accessed | tf_op | source)
XLA Modules:
  0.0 95.1 jit_solution(3538528672807740212)
XLA Ops:
  0.0 3.5 %gram.1 = f32[16,128,128]{2,1,0:T(8,128)S(1)} custom-call(s32[5]{0:T(128)} %order_ref.1, f32[512,640]{1,0:T(8,128)} %psi_ref.1), custom_call_target="tpu_custom_call" | custom-call | tf_op jit(solution)/shard_map/gram/pallas_call | solution.py:325
  3.6 20.5 %collective-permute-start = (f32[8,128,128]{2,1,0:T(8,128)S(1)}, f32[8,128,128]{2,1,0:T(8,128)S(1)}, u32[]{:S(2)}, u32[]{:S(2)}) collective-permute-start(f32[8,128,128]{2,1,0:T(8,128)S(1)} %dynamic-slice_bitcast_fusion), channel_id=1, source_target_pairs={{0,1},{1,0},{2,3},{3,2},{4,5},{5,4},{6,7},{7,6},{8,9},{9,8},{10,11... | collective-permute-start | bytes 1572872 | tf_op jit(solution)/shard_map/ppermute | solution.py:337
  24.1 1.5 %collective-permute-done = f32[8,128,128]{2,1,0:T(8,128)S(1)} collective-permute-done((f32[8,128,128]{2,1,0:T(8,128)S(1)}, f32[8,128,128]{2,1,0:T(8,128)S(1)}, u32[]{:S(2)}, u32[]{:S(2)}) %collective-permute-start) | collective-permute-done | bytes 524320 | tf_op jit(solution)/shard_map/ppermute | solution.py:337
  25.7 0.1 bitcast_add_fusion
  25.7 22.4 %all_to_all.10 = f32[64,16,128]{2,1,0:T(8,128)S(1)} all-to-all(f32[64,16,128]{2,1,0:T(8,128)S(1)} %bitcast.13), channel_id=1, replica_groups={{0,2,4,6,8,10,12,14,16,18,20,22,24,26,28,30,32,34,36,38,40,42,44,46,48,..., dimensions={0} | all-to-all | bytes 1048576 | tf_op jit(solution)/shard_map/all_to_all | solution.py:338
  48.1 0.1 reduce_sum.9
  48.3 23.0 %all_to_all.11 = f32[64,16,128]{2,1,0:T(8,128)S(1)} all-to-all(f32[64,16,128]{2,1,0:T(8,128)S(1)} %broadcast_in_dim.2), channel_id=1, replica_groups={{0,2,4,6,8,10,12,14,16,18,20,22,24,26,28,30,32,34,36,38,40,42,44,46,48,..., dimensions={0} | all-to-all | bytes 1048576 | tf_op jit(solution)/shard_map/all_to_all | solution.py:342
  71.3 3.9 %collective-permute-start.1 = (f32[8,128,128]{2,1,0:T(8,128)S(1)}, f32[8,128,128]{2,1,0:T(8,128)S(1)}, u32[]{:S(2)}, u32[]{:S(2)}) collective-permute-start(f32[8,128,128]{2,1,0:T(8,128)S(1)} %bitcast.8), channel_id=1, source_target_pairs={{0,1},{1,0},{2,3},{3,2},{4,5},{5,4},{6,7},{7,6},{8,9},{9,8},{10,11... | collective-permute-start | bytes 1572872 | tf_op jit(solution)/shard_map/ppermute | solution.py:345
  75.2 2.6 %lead.1.lead_ref = f32[128,128]{1,0:T(8,128)S(1)} custom-call(s32[1]{0:T(128)} %bitcast.core_ref, f32[8,128,128]{2,1,0:T(8,128)S(1)} %bitcast.9), custom_call_target="tpu_custom_call" | custom-call | tf_op jit(solution)/shard_map/lead/pallas_call | solution.py:350
  77.8 0.0 collective-permute-done.1.other_ref
  77.8 17.1 %finish.1 = f32[512,640]{1,0:T(8,128)} custom-call(s32[1]{0:T(128)} %bitcast.core_ref, s32[5]{0:T(128)} %order_ref.1, f32[128,128]{1,0:T(8,128)S(1)} %lead.1.lead_ref, f32[8,128,128]{2,1,0:T(8,128)S(1)} %bitcast.10, f32[8,128,128]{2,1,0:T(8,128)S(1)} %collective-permute-done.1.other_ref, f32[512,640]{1,0:T(8,128)} %psi_ref.1), custom_call_target="tpu_custom_call" | custom-call | tf_op jit(solution)/shard_map/finish/pallas_call | solution.py:363
  (2 shorter events, 0.1 us)
Async XLA Ops:
  3.6 22.1 %collective-permute-start = (f32[8,128,128]{2,1,0:T(8,128)S(1)}, f32[8,128,128]{2,1,0:T(8,128)S(1)}, u32[]{:S(2)}, u32[]{:S(2)}) collective-permute-start(f32[8,128,128]{2,1,0:T(8,128)S(1)} %dynamic-slice_bitcast_fusion), channel_id=1, source_target_pairs={{0,1},{1,0},{2,3},{3,2},{4,5},{5,4},{6,7},{7,6},{8,9},{9,8},{10,11... | collective-permute-start | bytes 1572872 | tf_op jit(solution)/shard_map/ppermute | solution.py:337
  71.3 6.5 %collective-permute-start.1 = (f32[8,128,128]{2,1,0:T(8,128)S(1)}, f32[8,128,128]{2,1,0:T(8,128)S(1)}, u32[]{:S(2)}, u32[]{:S(2)}) collective-permute-start(f32[8,128,128]{2,1,0:T(8,128)S(1)} %bitcast.8), channel_id=1, source_target_pairs={{0,1},{1,0},{2,3},{3,2},{4,5},{5,4},{6,7},{7,6},{8,9},{9,8},{10,11... | collective-permute-start | bytes 1572872 | tf_op jit(solution)/shard_map/ppermute | solution.py:345

commit v6 on v5

--- a/solution.py
+++ b/solution.py
@@ -52,15 +52,31 @@
     return copies
 
 
-def gram_kernel(scale, order_ref, psi_ref, out_ref, x_ref):
+def gram_half(scale, half, x_ref, out_ref):
+    first = half * (SLOTS // 2)
+    held = PAIRS[first:first + SLOTS // 2]
+    for i in range(NBLK):
+        js = [j for row, j in held if row == i]
+        if js:
+            row = dot_tn(x_ref[:, span(i, i + 1)], x_ref[:, span(js[0], js[-1] + 1)]) * scale
+            for at, j in enumerate(js):
+                out_ref[SLOT[i, j] - first] = row[:, span(at, at + 1)]
+    if half == 1:
+        lead = x_ref[:, span(0, 1)]
+        out_ref[SLOTS // 2 - 1] = dot_tn(lead, lead) * scale
+
+
+def send_kernel(scale, core_ref, order_ref, psi_ref, out_ref, x_ref):
     for i in range(NBLK):
         start = pl.multiple_of(order_ref[i] * BLOCK, BLOCK)
         x_ref[:, span(i, i + 1)] = psi_ref[:, pl.ds(start, BLOCK)]
-    for i in range(NBLK):
-        row = dot_tn(x_ref[:, span(i, i + 1)], x_ref[:, i * BLOCK:]) * scale
-        for j in range(i, NBLK):
-            out_ref[SLOT[i, j]] = row[:, span(j - i, j - i + 1)]
-    out_ref[SLOTS - 1] = out_ref[0]
+    for core in range(2):
+        pl.when(core_ref[0] == core)(lambda: gram_half(scale, 1 - core, x_ref, out_ref))
+
+
+def keep_kernel(scale, core_ref, x_ref, out_ref):
+    for core in range(2):
+        pl.when(core_ref[0] == core)(lambda: gram_half(scale, core, x_ref, out_ref))
 
 
 def eliminate(work_ref, col_ref, row_ref, after_panel):
@@ -322,18 +338,23 @@
     half = SLOTS // 2
     chunk = half * BLOCK // chips
 
-    gram = pl.pallas_call(
-        lambda *refs: gram_kernel(scale, *refs),
-        out_shape=pltpu.VMEM((SLOTS, BLOCK, BLOCK), jnp.float32),
+    core = core.astype(jnp.int32).reshape(1)
+    shape = (half, BLOCK, BLOCK)
+    send, x = pl.pallas_call(
+        lambda *refs: send_kernel(scale, *refs),
+        out_shape=[pltpu.VMEM(shape, jnp.float32), pltpu.VMEM((rows, bands), jnp.float32)],
+        in_specs=[smem(), smem(), vmem()],
+        out_specs=[vmem(), vmem()],
+        name="gram_send",
+    )(core, order, psi)
+    x = pltpu.with_memory_space_constraint(x, pltpu.VMEM)
+    keep = pl.pallas_call(
+        lambda *refs: keep_kernel(scale, *refs),
+        out_shape=pltpu.VMEM(shape, jnp.float32),
         in_specs=[smem(), vmem()],
         out_specs=vmem(),
-        scratch_shapes=[pltpu.VMEM((rows, bands), jnp.float32)],
-        name="gram",
-    )(order, psi)
-
-    gram = gram.reshape(2, half, BLOCK, BLOCK)
-    keep = lax.dynamic_index_in_dim(gram, core, 0, keepdims=False)
-    send = lax.dynamic_index_in_dim(gram, 1 - core, 0, keepdims=False)
+        name="gram_keep",
+    )(core, x)
     both = keep + lax.ppermute(send, "grid", pairs)
     parts = lax.all_to_all(
         both.reshape(chips, chunk, BLOCK), "grid", 0, 0, axis_index_groups=groups, tiled=True
@@ -346,7 +367,6 @@
     mine = pltpu.with_memory_space_constraint(mine, pltpu.VMEM)
     other = pltpu.with_memory_space_constraint(other, pltpu.VMEM)
 
-    core = core.astype(jnp.int32).reshape(1)
     lead = pl.pallas_call(
         lead_kernel,
         out_shape=pltpu.VMEM((BLOCK, BLOCK), jnp.float32),

time: 95.3 us -> 94.8 us (level)
  waiting for transfers between devices: 1.54 us -> 0.01 us
    ppermute x1, waiting for transfers between devices: 1.54 us -> 0.01 us  [local(): both = keep + lax.ppermute(send, 'grid', pairs)]
    pallas_call x1 -> x2, Pallas kernels: 3.53 us -> 4.29 us  [the longest x1 2.74 us: local(): pl.pallas_call(lambda *refs: send_kernel(scale, *refs), out_shape=[pltpu....]
  transfers between devices with their start and end apart: 2 -> 2, of which waited for: 1 -> 0; matrix products, arithmetic and copies ran while one was open for 0% -> 0% of each run, Pallas kernels for 3% -> 4%
where the time goes in v6:
time: 94.8 us; the launch traced here: 94.6 us
  blocking collectives  45.5 us (48%)
  starting transfers between devices  24.7 us (26%)
  Pallas kernels  24.1 us (25%)
    all_to_all x1, blocking collectives, local(): lax.all_to_all(jnp.broadcast_to(total[None], parts.shape), 'grid', 0, 0,...  23 us
    all_to_all x1, blocking collectives, local(): lax.all_to_all(both.reshape(chips, chunk, BLOCK), 'grid', 0, 0, axis_inde...  22.4 us
    ppermute x1, starting transfers between devices, local(): both = keep + lax.ppermute(send, 'grid', pairs)  20.8 us
    pallas_call x1, Pallas kernels, local(): pl.pallas_call(finish_kernel, out_shape=jax.ShapeDtypeStruct((rows, bands...  17.1 us
    ppermute x1, starting transfers between devices, local(): other = lax.ppermute(mine, 'grid', pairs)  3.88 us
    pallas_call x1, Pallas kernels, local(): pl.pallas_call(lambda *refs: send_kernel(scale, *refs), out_shape=[pltpu....  2.74 us
    pallas_call x1, Pallas kernels, local(): pl.pallas_call(lead_kernel, out_shape=pltpu.VMEM((BLOCK, BLOCK), jnp.floa...  2.64 us
  transfers between devices with their start and end apart: 2, of which 0 were waited for; matrix products, arithmetic and copies ran while one was open for 0% of the time, Pallas kernels for 4%

profile of v6, /device:TPU:513, one launch (start us, length us, event | category | flops | bytes accessed | tf_op | source)
XLA Modules:
  0.0 94.6 jit_solution(1692859347436918279)
XLA Ops:
  0.0 2.7 %gram_send.1 = (f32[8,128,128]{2,1,0:T(8,128)S(1)}, f32[512,640]{1,0:T(8,128)S(1)}) custom-call(s32[1]{0:T(128)} %bitcast.refs_0_.core_ref, s32[5]{0:T(128)} %order_ref.1, f32[512,640]{1,0:T(8,128)} %psi_ref.1), custom_call_target="tpu_custom_call" | custom-call | tf_op jit(solution)/shard_map/gram_send/pallas_call | solution.py:343
  2.7 20.8 %collective-permute-start = (f32[8,128,128]{2,1,0:T(8,128)S(1)}, f32[8,128,128]{2,1,0:T(8,128)S(1)}, u32[]{:S(2)}, u32[]{:S(2)}) collective-permute-start(f32[8,128,128]{2,1,0:T(8,128)S(1)} %get-tuple-element.8), channel_id=1, source_target_pairs={{0,1},{1,0},{2,3},{3,2},{4,5},{5,4},{6,7},{7,6},{8,9},{9,8},{10,11... | collective-permute-start | bytes 1572872 | tf_op jit(solution)/shard_map/ppermute | solution.py:358
  23.5 1.6 %gram_keep.1 = f32[8,128,128]{2,1,0:T(8,128)S(1)} custom-call(s32[1]{0:T(128)} %bitcast.refs_0_.core_ref, f32[512,640]{1,0:T(8,128)S(1)} %get-tuple-element.7.refs_1_), custom_call_target="tpu_custom_call" | custom-call | tf_op jit(solution)/shard_map/gram_keep/pallas_call | solution.py:351
  25.1 0.0 collective-permute-done
  25.1 0.1 add.8
  25.2 22.4 %all_to_all.10 = f32[64,16,128]{2,1,0:T(8,128)S(1)} all-to-all(f32[64,16,128]{2,1,0:T(8,128)S(1)} %bitcast.6), channel_id=1, replica_groups={{0,2,4,6,8,10,12,14,16,18,20,22,24,26,28,30,32,34,36,38,40,42,44,46,48,..., dimensions={0} | all-to-all | bytes 1048576 | tf_op jit(solution)/shard_map/all_to_all | solution.py:359
  47.6 0.1 reduce_sum.9
  47.7 23.0 %all_to_all.11 = f32[64,16,128]{2,1,0:T(8,128)S(1)} all-to-all(f32[64,16,128]{2,1,0:T(8,128)S(1)} %broadcast_in_dim.2), channel_id=1, replica_groups={{0,2,4,6,8,10,12,14,16,18,20,22,24,26,28,30,32,34,36,38,40,42,44,46,48,..., dimensions={0} | all-to-all | bytes 1048576 | tf_op jit(solution)/shard_map/all_to_all | solution.py:363
  70.7 3.9 %collective-permute-start.1 = (f32[8,128,128]{2,1,0:T(8,128)S(1)}, f32[8,128,128]{2,1,0:T(8,128)S(1)}, u32[]{:S(2)}, u32[]{:S(2)}) collective-permute-start(f32[8,128,128]{2,1,0:T(8,128)S(1)} %bitcast.3), channel_id=1, source_target_pairs={{0,1},{1,0},{2,3},{3,2},{4,5},{5,4},{6,7},{7,6},{8,9},{9,8},{10,11... | collective-permute-start | bytes 1572872 | tf_op jit(solution)/shard_map/ppermute | solution.py:366
  74.6 2.6 %lead.1.lead_ref = f32[128,128]{1,0:T(8,128)S(1)} custom-call(s32[1]{0:T(128)} %bitcast.refs_0_.core_ref, f32[8,128,128]{2,1,0:T(8,128)S(1)} %bitcast.4), custom_call_target="tpu_custom_call" | custom-call | tf_op jit(solution)/shard_map/lead/pallas_call | solution.py:370
  77.3 0.0 collective-permute-done.1.other_ref
  77.3 17.1 %finish.1 = f32[512,640]{1,0:T(8,128)} custom-call(s32[1]{0:T(128)} %bitcast.refs_0_.core_ref, s32[5]{0:T(128)} %order_ref.1, f32[128,128]{1,0:T(8,128)S(1)} %lead.1.lead_ref, f32[8,128,128]{2,1,0:T(8,128)S(1)} %bitcast.5, f32[8,128,128]{2,1,0:T(8,128)S(1)} %collective-permute-done.1.other_ref, f32[512,640]{1,0:T(8,128)} %psi_ref.1), custom_call_target="tpu_custom_call" | custom-call | tf_op jit(solution)/shard_map/finish/pallas_call | solution.py:383
  (1 shorter events, 0.0 us)
Async XLA Ops:
  2.7 22.3 %collective-permute-start = (f32[8,128,128]{2,1,0:T(8,128)S(1)}, f32[8,128,128]{2,1,0:T(8,128)S(1)}, u32[]{:S(2)}, u32[]{:S(2)}) collective-permute-start(f32[8,128,128]{2,1,0:T(8,128)S(1)} %get-tuple-element.8), channel_id=1, source_target_pairs={{0,1},{1,0},{2,3},{3,2},{4,5},{5,4},{6,7},{7,6},{8,9},{9,8},{10,11... | collective-permute-start | bytes 1572872 | tf_op jit(solution)/shard_map/ppermute | solution.py:358
  70.7 6.5 %collective-permute-start.1 = (f32[8,128,128]{2,1,0:T(8,128)S(1)}, f32[8,128,128]{2,1,0:T(8,128)S(1)}, u32[]{:S(2)}, u32[]{:S(2)}) collective-permute-start(f32[8,128,128]{2,1,0:T(8,128)S(1)} %bitcast.3), channel_id=1, source_target_pairs={{0,1},{1,0},{2,3},{3,2},{4,5},{5,4},{6,7},{7,6},{8,9},{9,8},{10,11... | collective-permute-start | bytes 1572872 | tf_op jit(solution)/shard_map/ppermute | solution.py:366

commit v7 on v6

--- a/solution.py
+++ b/solution.py
@@ -13,6 +13,7 @@
 PAIRS = [(i, j) for i in range(NBLK) for j in range(i, NBLK)]
 SLOT = {pair: slot for slot, pair in enumerate(PAIRS)}
 SLOTS = 16
+LOADS = 4
 HIGHEST = lax.Precision.HIGHEST
 
 
@@ -66,10 +67,20 @@
         out_ref[SLOTS // 2 - 1] = dot_tn(lead, lead) * scale
 
 
-def send_kernel(scale, core_ref, order_ref, psi_ref, out_ref, x_ref):
-    for i in range(NBLK):
-        start = pl.multiple_of(order_ref[i] * BLOCK, BLOCK)
-        x_ref[:, span(i, i + 1)] = psi_ref[:, pl.ds(start, BLOCK)]
+def send_kernel(scale, core_ref, order_ref, psi_ref, out_ref, x_ref, raw_ref, sems):
+    rows = psi_ref.shape[0] // LOADS
+    parts = [slice(t * rows, (t + 1) * rows) for t in range(LOADS)]
+    loads = [
+        pltpu.make_async_copy(psi_ref.at[part], raw_ref.at[part], sems.at[t])
+        for t, part in enumerate(parts)
+    ]
+    for load in loads:
+        load.start()
+    starts = [pl.multiple_of(order_ref[i] * BLOCK, BLOCK) for i in range(NBLK)]
+    for part, load in zip(parts, loads):
+        load.wait()
+        for i, start in enumerate(starts):
+            x_ref[part, span(i, i + 1)] = raw_ref[part, pl.ds(start, BLOCK)]
     for core in range(2):
         pl.when(core_ref[0] == core)(lambda: gram_half(scale, 1 - core, x_ref, out_ref))
 
@@ -343,8 +354,12 @@
     send, x = pl.pallas_call(
         lambda *refs: send_kernel(scale, *refs),
         out_shape=[pltpu.VMEM(shape, jnp.float32), pltpu.VMEM((rows, bands), jnp.float32)],
-        in_specs=[smem(), smem(), vmem()],
+        in_specs=[smem(), smem(), anywhere()],
         out_specs=[vmem(), vmem()],
+        scratch_shapes=[
+            pltpu.VMEM((rows, bands), jnp.float32),
+            pltpu.SemaphoreType.DMA((LOADS,)),
+        ],
         name="gram_send",
     )(core, order, psi)
     x = pltpu.with_memory_space_constraint(x, pltpu.VMEM)

time: 94.8 us -> 95.4 us (level)
  no operation moved by 1% of the time
where the time goes in v7:
time: 95.4 us; the launch traced here: 95.1 us
  blocking collectives  45.5 us (48%)
  starting transfers between devices  24.7 us (26%)
  Pallas kernels  24.6 us (26%)
    all_to_all x1, blocking collectives, local(): lax.all_to_all(jnp.broadcast_to(total[None], parts.shape), 'grid', 0, 0,...  23 us
    all_to_all x1, blocking collectives, local(): lax.all_to_all(both.reshape(chips, chunk, BLOCK), 'grid', 0, 0, axis_inde...  22.4 us
    ppermute x1, starting transfers between devices, local(): both = keep + lax.ppermute(send, 'grid', pairs)  20.8 us
    pallas_call x1, Pallas kernels, local(): pl.pallas_call(finish_kernel, out_shape=jax.ShapeDtypeStruct((rows, bands...  17.1 us
    ppermute x1, starting transfers between devices, local(): other = lax.ppermute(mine, 'grid', pairs)  3.88 us
    pallas_call x1, Pallas kernels, local(): pl.pallas_call(lambda *refs: send_kernel(scale, *refs), out_shape=[pltpu....  3.31 us
    pallas_call x1, Pallas kernels, local(): pl.pallas_call(lead_kernel, out_shape=pltpu.VMEM((BLOCK, BLOCK), jnp.floa...  2.64 us
  transfers between devices with their start and end apart: 2, of which 0 were waited for; matrix products, arithmetic and copies ran while one was open for 0% of the time, Pallas kernels for 4%

profile of v7, /device:TPU:513, one launch (start us, length us, event | category | flops | bytes accessed | tf_op | source)
XLA Modules:
  0.0 95.1 jit_solution(5818983864467568984)
XLA Ops:
  0.0 3.3 %gram_send.1 = (f32[8,128,128]{2,1,0:T(8,128)S(1)}, f32[512,640]{1,0:T(8,128)S(1)}) custom-call(s32[1]{0:T(128)} %bitcast.refs_0_.core_ref, s32[5]{0:T(128)} %order_ref.1, f32[512,640]{1,0:T(8,128)} %psi_ref.1), custom_call_target="tpu_custom_call" | custom-call | tf_op jit(solution)/shard_map/gram_send/pallas_call | solution.py:354
  3.3 20.8 %collective-permute-start = (f32[8,128,128]{2,1,0:T(8,128)S(1)}, f32[8,128,128]{2,1,0:T(8,128)S(1)}, u32[]{:S(2)}, u32[]{:S(2)}) collective-permute-start(f32[8,128,128]{2,1,0:T(8,128)S(1)} %get-tuple-element.8), channel_id=1, source_target_pairs={{0,1},{1,0},{2,3},{3,2},{4,5},{5,4},{6,7},{7,6},{8,9},{9,8},{10,11... | collective-permute-start | bytes 1572872 | tf_op jit(solution)/shard_map/ppermute | solution.py:373
  24.1 1.6 %gram_keep.1 = f32[8,128,128]{2,1,0:T(8,128)S(1)} custom-call(s32[1]{0:T(128)} %bitcast.refs_0_.core_ref, f32[512,640]{1,0:T(8,128)S(1)} %get-tuple-element.7.refs_1_), custom_call_target="tpu_custom_call" | custom-call | tf_op jit(solution)/shard_map/gram_keep/pallas_call | solution.py:366
  25.7 0.0 collective-permute-done
  25.7 0.1 add.8
  25.7 22.4 %all_to_all.10 = f32[64,16,128]{2,1,0:T(8,128)S(1)} all-to-all(f32[64,16,128]{2,1,0:T(8,128)S(1)} %bitcast.6), channel_id=1, replica_groups={{0,2,4,6,8,10,12,14,16,18,20,22,24,26,28,30,32,34,36,38,40,42,44,46,48,..., dimensions={0} | all-to-all | bytes 1048576 | tf_op jit(solution)/shard_map/all_to_all | solution.py:374
  48.1 0.1 reduce_sum.9
  48.3 23.0 %all_to_all.11 = f32[64,16,128]{2,1,0:T(8,128)S(1)} all-to-all(f32[64,16,128]{2,1,0:T(8,128)S(1)} %broadcast_in_dim.2), channel_id=1, replica_groups={{0,2,4,6,8,10,12,14,16,18,20,22,24,26,28,30,32,34,36,38,40,42,44,46,48,..., dimensions={0} | all-to-all | bytes 1048576 | tf_op jit(solution)/shard_map/all_to_all | solution.py:378
  71.3 3.9 %collective-permute-start.1 = (f32[8,128,128]{2,1,0:T(8,128)S(1)}, f32[8,128,128]{2,1,0:T(8,128)S(1)}, u32[]{:S(2)}, u32[]{:S(2)}) collective-permute-start(f32[8,128,128]{2,1,0:T(8,128)S(1)} %bitcast.3), channel_id=1, source_target_pairs={{0,1},{1,0},{2,3},{3,2},{4,5},{5,4},{6,7},{7,6},{8,9},{9,8},{10,11... | collective-permute-start | bytes 1572872 | tf_op jit(solution)/shard_map/ppermute | solution.py:381
  75.2 2.6 %lead.1.lead_ref = f32[128,128]{1,0:T(8,128)S(1)} custom-call(s32[1]{0:T(128)} %bitcast.refs_0_.core_ref, f32[8,128,128]{2,1,0:T(8,128)S(1)} %bitcast.4), custom_call_target="tpu_custom_call" | custom-call | tf_op jit(solution)/shard_map/lead/pallas_call | solution.py:385
  77.8 0.0 collective-permute-done.1.other_ref
  77.8 17.1 %finish.1 = f32[512,640]{1,0:T(8,128)} custom-call(s32[1]{0:T(128)} %bitcast.refs_0_.core_ref, s32[5]{0:T(128)} %order_ref.1, f32[128,128]{1,0:T(8,128)S(1)} %lead.1.lead_ref, f32[8,128,128]{2,1,0:T(8,128)S(1)} %bitcast.5, f32[8,128,128]{2,1,0:T(8,128)S(1)} %collective-permute-done.1.other_ref, f32[512,640]{1,0:T(8,128)} %psi_ref.1), custom_call_target="tpu_custom_call" | custom-call | tf_op jit(solution)/shard_map/finish/pallas_call | solution.py:398
  (1 shorter events, 0.0 us)
Async XLA Ops:
  3.3 22.3 %collective-permute-start = (f32[8,128,128]{2,1,0:T(8,128)S(1)}, f32[8,128,128]{2,1,0:T(8,128)S(1)}, u32[]{:S(2)}, u32[]{:S(2)}) collective-permute-start(f32[8,128,128]{2,1,0:T(8,128)S(1)} %get-tuple-element.8), channel_id=1, source_target_pairs={{0,1},{1,0},{2,3},{3,2},{4,5},{5,4},{6,7},{7,6},{8,9},{9,8},{10,11... | collective-permute-start | bytes 1572872 | tf_op jit(solution)/shard_map/ppermute | solution.py:373
  71.3 6.5 %collective-permute-start.1 = (f32[8,128,128]{2,1,0:T(8,128)S(1)}, f32[8,128,128]{2,1,0:T(8,128)S(1)}, u32[]{:S(2)}, u32[]{:S(2)}) collective-permute-start(f32[8,128,128]{2,1,0:T(8,128)S(1)} %bitcast.3), channel_id=1, source_target_pairs={{0,1},{1,0},{2,3},{3,2},{4,5},{5,4},{6,7},{7,6},{8,9},{9,8},{10,11... | collective-permute-start | bytes 1572872 | tf_op jit(solution)/shard_map/ppermute | solution.py:381
